TPU v7x, 8 devices: a whole 2x2x1 slice. The times are simulated.
8 devices in a mesh: gz: 2 (over z, y), gy: 2 (over x), gx: 2 (over core).
Axes of the slice: x: 2, y: 2, z: 1, core: 2. Of those that a mesh axis runs over, the one named last changes fastest.
Arguments:
- k_cell: float32 [144, 144, 144], P('gx', 'gy', 'gz')
- k_ghost: float32 [6, 144, 144], replicated
- f_rhs: float32 [144, 144, 144], P('gx', 'gy', 'gz')
- u_init: float32 [144, 144, 144], P('gx', 'gy', 'gz')
Outputs:
- output 1: float32 [144, 144, 144], P('gx', 'gy', 'gz')
- output 2: float32 [144, 144, 144], P('gx', 'gy', 'gz')
- output 3: float32 [8], replicated
All inputs are finite; a program needn't handle non-finite values.
Results may differ from a plain program's by a relative error of at most 0.001.
Values sent between devices are 32-bit elements.
A program may use at most 1 GiB of HBM per device.

v0:
```python
import jax
import jax.numpy as jnp
from jax import lax
from jax.sharding import PartitionSpec as P

CG_ITERS = 8
GRID_AXES = ('gx', 'gy', 'gz')
MESH_AXES = ('gz', 'gy', 'gx')


def neighbour_layers(grid_field, axis_dim, axis_len):
    size_here = grid_field.shape[axis_dim]
    low_layer = lax.slice_in_dim(grid_field, 0, 1, axis=axis_dim)
    top_layer = lax.slice_in_dim(grid_field, size_here - 1, size_here, axis=axis_dim)
    if axis_len == 1:
        return jnp.zeros_like(top_layer), jnp.zeros_like(low_layer)
    upward = [(src_rank, src_rank + 1) for src_rank in range(axis_len - 1)]
    downward = [(src_rank + 1, src_rank) for src_rank in range(axis_len - 1)]
    from_below = lax.ppermute(top_layer, GRID_AXES[axis_dim], upward)
    from_above = lax.ppermute(low_layer, GRID_AXES[axis_dim], downward)
    return from_below, from_above


def harmonic_faces(k_ext, axis_dim):
    size_here = k_ext.shape[axis_dim]
    left_k = lax.slice_in_dim(k_ext, 0, size_here - 1, axis=axis_dim)
    right_k = lax.slice_in_dim(k_ext, 1, size_here, axis=axis_dim)
    return 2.0 * left_k * right_k / (left_k + right_k)


def apply_operator(grid_field, face_coefs, layers):
    op_total = None
    for axis_dim in range(3):
        from_below, from_above = layers[axis_dim]
        padded = jnp.concatenate([from_below, grid_field, from_above], axis=axis_dim)
        size_here = padded.shape[axis_dim]
        face_flux = face_coefs[axis_dim] * (lax.slice_in_dim(padded, 1, size_here, axis=axis_dim) - lax.slice_in_dim(padded, 0, size_here - 1, axis=axis_dim))
        axis_part = lax.slice_in_dim(face_flux, 0, size_here - 2, axis=axis_dim) - lax.slice_in_dim(face_flux, 1, size_here - 1, axis=axis_dim)
        op_total = axis_part if op_total is None else op_total + axis_part
    return op_total


def diagonal(face_coefs):
    diag_sum = None
    for axis_dim in range(3):
        size_here = face_coefs[axis_dim].shape[axis_dim]
        low_coef = lax.slice_in_dim(face_coefs[axis_dim], 0, size_here - 1, axis=axis_dim)
        high_coef = lax.slice_in_dim(face_coefs[axis_dim], 1, size_here, axis=axis_dim)
        diag_sum = low_coef + high_coef if diag_sum is None else diag_sum + low_coef + high_coef
    return diag_sum


def local_coefs(k_cell, k_ghost, coords, counts):
    block_shape = k_cell.shape
    face_coefs = []
    for axis_dim in range(3):
        others = [other_dim for other_dim in range(3) if other_dim != axis_dim]
        starts = (coords[others[0]] * block_shape[others[0]], coords[others[1]] * block_shape[others[1]])
        extent = (block_shape[others[0]], block_shape[others[1]])
        low_wall = jnp.expand_dims(lax.dynamic_slice(k_ghost[2 * axis_dim], starts, extent), axis_dim)
        high_wall = jnp.expand_dims(lax.dynamic_slice(k_ghost[2 * axis_dim + 1], starts, extent), axis_dim)
        from_below, from_above = neighbour_layers(k_cell, axis_dim, counts[axis_dim])
        from_below = jnp.where(coords[axis_dim] == 0, low_wall, from_below)
        from_above = jnp.where(coords[axis_dim] == counts[axis_dim] - 1, high_wall, from_above)
        face_coefs.append(harmonic_faces(jnp.concatenate([from_below, k_cell, from_above], axis=axis_dim), axis_dim))
    return face_coefs


def solution(mesh):
    counts = tuple(mesh.shape[axis_name] for axis_name in GRID_AXES)
    grid_spec = P('gx', 'gy', 'gz')

    def global_sum(local_value):
        return lax.psum(local_value, MESH_AXES)

    def local_solve(k_cell, k_ghost, f_rhs, u_init):
        coords = [lax.axis_index(axis_name) for axis_name in GRID_AXES]
        face_coefs = local_coefs(k_cell, k_ghost, coords, counts)
        inv_diag = 1.0 / diagonal(face_coefs)

        def apply_stencil(grid_field):
            layers = [neighbour_layers(grid_field, axis_dim, counts[axis_dim]) for axis_dim in range(3)]
            return apply_operator(grid_field, face_coefs, layers)

        residual = f_rhs - apply_stencil(u_init)
        precond = residual * inv_diag
        rz_old = global_sum(jnp.sum(residual * precond))
        approx = u_init
        direction = precond
        history = []
        for iteration in range(CG_ITERS):
            q_vec = apply_stencil(direction)
            step_alpha = rz_old / global_sum(jnp.sum(direction * q_vec))
            approx = approx + step_alpha * direction
            residual = residual - step_alpha * q_vec
            precond = residual * inv_diag
            pair_sums = global_sum(jnp.stack([jnp.sum(residual * precond), jnp.sum(residual * residual)]))
            direction = precond + (pair_sums[0] / rz_old) * direction
            rz_old = pair_sums[0]
            history.append(pair_sums[1])
        return approx, residual, jnp.stack(history)

    return jax.shard_map(local_solve, mesh=mesh, in_specs=(grid_spec, P(), grid_spec, grid_spec), out_specs=(grid_spec, grid_spec, P()), check_vma=False)
```

profile of v0, /device:TPU:0, one launch (start us, length us, event | category | flops | bytes accessed | tf_op | source)
XLA Modules:
  0.0 954.6 jit_solution(16701900792967236266)
XLA Ops:
  98.4 13.2 %fusion.56 = (f32[72,72,72]{2,0,1:T(8,128)S(1)}, f32[72,72,72]{2,0,1:T(8,128)}, f32[72,72,72]{2,0,1:T(8,128)}) fusion(f32[72,72,73]{2,0,1:T(8,128)S(1)} %get-tuple-element.68, f32[72,73,72]{2,0,1:T(8,128)S(1)} %get-tuple-element.66, f32[73,72,72]{2,0,1:T(8,128)} %get-tuple-element.70, f32[72,72,73]{2,0,1:T(8,128)} %get-tuple-element.67, ...), kind=kLoop, calls=%fused_computation.173 | loop fusion | flops 4852224 | bytes 23887872 | tf_op jit(solution)/shard_map/mul | solution.py:86
  156.6 22.5 %all-reduce = (f32[]{:T(128)}, f32[]{:T(128)}) all-reduce(f32[]{:T(128)} %get-tuple-element.29, f32[]{:T(128)} %get-tuple-element.28), channel_id=1, replica_groups=mesh['gz'=2,'gy'=2,'gx'=2] {'gz','gy','gx'}, use_global_device_ids=true, to_apply=%region_1.2 | all-reduce | flops 2 | bytes 16 | tf_op jit(solution)/shard_map/psum | solution.py:74
  188.2 22.7 %psum.121 = f32[2]{0:T(128)S(1)} all-reduce(f32[2]{0:T(128)S(1)} %pad_maximum_fusion.6), channel_id=1, replica_groups=mesh['gz'=2,'gy'=2,'gx'=2] {'gz','gy','gx'}, use_global_device_ids=true, to_apply=%region_6.7 | all-reduce | flops 2 | bytes 16 | tf_op jit(solution)/shard_map/psum | solution.py:74
  259.8 22.4 %psum.122 = f32[]{:T(128)} all-reduce(f32[]{:T(128)} %get-tuple-element.57), channel_id=1, replica_groups=mesh['gz'=2,'gy'=2,'gx'=2] {'gz','gy','gx'}, use_global_device_ids=true, to_apply=%region_8.9 | all-reduce | flops 1 | bytes 8 | tf_op jit(solution)/shard_map/psum | solution.py:74
  283.7 7.2 multiply_reduce_fusion.18
  292.1 22.8 %psum.123 = f32[2]{0:T(128)S(1)} all-reduce(f32[2]{0:T(128)S(1)} %pad_maximum_fusion.7), channel_id=1, replica_groups=mesh['gz'=2,'gy'=2,'gx'=2] {'gz','gy','gx'}, use_global_device_ids=true, to_apply=%region_11.12 | all-reduce | flops 2 | bytes 16 | tf_op jit(solution)/shard_map/psum | solution.py:74
  362.9 22.4 %psum.124 = f32[]{:T(128)} all-reduce(f32[]{:T(128)} %get-tuple-element.53), channel_id=1, replica_groups=mesh['gz'=2,'gy'=2,'gx'=2] {'gz','gy','gx'}, use_global_device_ids=true, to_apply=%region_13.14 | all-reduce | flops 1 | bytes 8 | tf_op jit(solution)/shard_map/psum | solution.py:74
  386.7 7.1 multiply_reduce_fusion.15
  395.2 22.7 %psum.125 = f32[2]{0:T(128)S(1)} all-reduce(f32[2]{0:T(128)S(1)} %pad_maximum_fusion.8), channel_id=1, replica_groups=mesh['gz'=2,'gy'=2,'gx'=2] {'gz','gy','gx'}, use_global_device_ids=true, to_apply=%region_16.17 | all-reduce | flops 2 | bytes 16 | tf_op jit(solution)/shard_map/psum | solution.py:74
  465.9 22.4 %psum.126 = f32[]{:T(128)} all-reduce(f32[]{:T(128)} %get-tuple-element.49), channel_id=1, replica_groups=mesh['gz'=2,'gy'=2,'gx'=2] {'gz','gy','gx'}, use_global_device_ids=true, to_apply=%region_18.19 | all-reduce | flops 1 | bytes 8 | tf_op jit(solution)/shard_map/psum | solution.py:74
  489.6 7.2 multiply_reduce_fusion.12
  498.3 22.7 %psum.127 = f32[2]{0:T(128)S(1)} all-reduce(f32[2]{0:T(128)S(1)} %pad_maximum_fusion.9), channel_id=1, replica_groups=mesh['gz'=2,'gy'=2,'gx'=2] {'gz','gy','gx'}, use_global_device_ids=true, to_apply=%region_21.22 | all-reduce | flops 2 | bytes 16 | tf_op jit(solution)/shard_map/psum | solution.py:74
  569.2 22.4 %psum.128 = f32[]{:T(128)} all-reduce(f32[]{:T(128)} %get-tuple-element.45), channel_id=1, replica_groups=mesh['gz'=2,'gy'=2,'gx'=2] {'gz','gy','gx'}, use_global_device_ids=true, to_apply=%region_23.24 | all-reduce | flops 1 | bytes 8 | tf_op jit(solution)/shard_map/psum | solution.py:74
  593.0 7.1 multiply_reduce_fusion.9
  601.4 22.7 %psum.129 = f32[2]{0:T(128)S(1)} all-reduce(f32[2]{0:T(128)S(1)} %pad_maximum_fusion.10), channel_id=1, replica_groups=mesh['gz'=2,'gy'=2,'gx'=2] {'gz','gy','gx'}, use_global_device_ids=true, to_apply=%region_26.27 | all-reduce | flops 2 | bytes 16 | tf_op jit(solution)/shard_map/psum | solution.py:74
  672.1 22.4 %psum.130 = f32[]{:T(128)} all-reduce(f32[]{:T(128)} %get-tuple-element.41), channel_id=1, replica_groups=mesh['gz'=2,'gy'=2,'gx'=2] {'gz','gy','gx'}, use_global_device_ids=true, to_apply=%region_28.29 | all-reduce | flops 1 | bytes 8 | tf_op jit(solution)/shard_map/psum | solution.py:74
  695.8 7.1 multiply_reduce_fusion.6
  704.1 22.7 %psum.131 = f32[2]{0:T(128)S(1)} all-reduce(f32[2]{0:T(128)S(1)} %pad_maximum_fusion.11), channel_id=1, replica_groups=mesh['gz'=2,'gy'=2,'gx'=2] {'gz','gy','gx'}, use_global_device_ids=true, to_apply=%region_31.32 | all-reduce | flops 2 | bytes 16 | tf_op jit(solution)/shard_map/psum | solution.py:74
  774.6 22.4 %psum.132 = f32[]{:T(128)} all-reduce(f32[]{:T(128)} %get-tuple-element.37), channel_id=1, replica_groups=mesh['gz'=2,'gy'=2,'gx'=2] {'gz','gy','gx'}, use_global_device_ids=true, to_apply=%region_33.34 | all-reduce | flops 1 | bytes 8 | tf_op jit(solution)/shard_map/psum | solution.py:74
  798.4 7.1 multiply_reduce_fusion.3
  806.9 22.7 %psum.133 = f32[2]{0:T(128)S(1)} all-reduce(f32[2]{0:T(128)S(1)} %pad_maximum_fusion.12), channel_id=1, replica_groups=mesh['gz'=2,'gy'=2,'gx'=2] {'gz','gy','gx'}, use_global_device_ids=true, to_apply=%region_36.37 | all-reduce | flops 2 | bytes 16 | tf_op jit(solution)/shard_map/psum | solution.py:74
  880.9 22.4 %psum.134 = f32[]{:T(128)} all-reduce(f32[]{:T(128)} %get-tuple-element.33), channel_id=1, replica_groups=mesh['gz'=2,'gy'=2,'gx'=2] {'gz','gy','gx'}, use_global_device_ids=true, to_apply=%region_38.39 | all-reduce | flops 1 | bytes 8 | tf_op jit(solution)/shard_map/psum | solution.py:74
  904.6 10.1 %multiply_add_fusion = f32[72,72,72]{2,0,1:T(8,128)} fusion(f32[72,72,72]{2,0,1:T(8,128)} %copy-done.19, f32[72,72,72]{2,0,1:T(8,128)} %copy-done.14, f32[72,72,72]{2,0,1:T(8,128)} %copy-done.12, f32[72,72,72]{2,0,1:T(8,128)} %copy-done.10, f32[72,72,72]{2,0,1:T(8,128)} %copy-done.8, f32[72,72,72]{2,0,1:T(8,128)} %copy-done.6, ...), kind=kLoop, calls=%fused_computation.118 | loop fusion | flops 5971968 | bytes 14929952 | tf_op jit(solution)/shard_map/add | solution.py:94
  925.2 22.7 %psum.135 = f32[2]{0:T(128)S(1)} all-reduce(f32[2]{0:T(128)S(1)} %pad_maximum_fusion.13), channel_id=1, replica_groups=mesh['gz'=2,'gy'=2,'gx'=2] {'gz','gy','gx'}, use_global_device_ids=true, to_apply=%region_41.42 | all-reduce | flops 2 | bytes 16 | tf_op jit(solution)/shard_map/psum | solution.py:74
  (354 shorter events, 505.4 us)
Async XLA Ops:
  9.7 59.2 %collective-permute-start.10 = (f32[72,72,1]{1,0,2:T(8,128)}, f32[72,72,1]{1,0,2:T(8,128)}, u32[]{:S(2)}, u32[]{:S(2)}) collective-permute-start(f32[72,72,1]{1,0,2:T(8,128)} %copy.145), channel_id=1, source_target_pairs={{4,0},{5,1},{6,2},{7,3}} | collective-permute-start | bytes 62216 | tf_op jit(solution)/shard_map/ppermute | solution.py:20
  14.2 61.0 %collective-permute-start.11 = (f32[72,72,1]{1,0,2:T(8,128)}, f32[72,72,1]{1,0,2:T(8,128)}, u32[]{:S(2)}, u32[]{:S(2)}) collective-permute-start(f32[72,72,1]{1,0,2:T(8,128)} %copy.146), channel_id=1, source_target_pairs={{0,4},{1,5},{2,6},{3,7}} | collective-permute-start | bytes 62216 | tf_op jit(solution)/shard_map/ppermute | solution.py:19
  27.2 19.4 %collective-permute-start.9 = (f32[72,72,1]{1,0,2:T(8,128)}, f32[72,72,1]{1,0,2:T(8,128)}, u32[]{:S(2)}, u32[]{:S(2)}) collective-permute-start(f32[72,72,1]{1,0,2:T(8,128)} %copy.144), channel_id=1, source_target_pairs={{4,0},{5,1},{6,2},{7,3}} | collective-permute-start | bytes 62216 | tf_op jit(solution)/shard_map/ppermute | solution.py:20
  31.7 21.0 %collective-permute-start.8 = (f32[72,72,1]{1,0,2:T(8,128)}, f32[72,72,1]{1,0,2:T(8,128)}, u32[]{:S(2)}, u32[]{:S(2)}) collective-permute-start(f32[72,72,1]{1,0,2:T(8,128)} %copy.143), channel_id=1, source_target_pairs={{0,4},{1,5},{2,6},{3,7}} | collective-permute-start | bytes 62216 | tf_op jit(solution)/shard_map/ppermute | solution.py:19
  38.9 40.6 %collective-permute-start.6 = (f32[72,1,72]{2,0,1:T(8,128)}, f32[72,1,72]{2,0,1:T(8,128)}, u32[]{:S(2)}, u32[]{:S(2)}) collective-permute-start(f32[72,1,72]{2,0,1:T(8,128)} %get-tuple-element.126), channel_id=1, source_target_pairs={{2,0},{3,1},{6,4},{7,5}} | collective-permute-start | bytes 62216 | tf_op jit(solution)/shard_map/ppermute | solution.py:20
  46.6 36.7 %collective-permute-start.7 = (f32[72,1,72]{2,0,1:T(8,128)}, f32[72,1,72]{2,0,1:T(8,128)S(1)}, u32[]{:S(2)}, u32[]{:S(2)}) collective-permute-start(f32[72,1,72]{2,0,1:T(8,128)} %get-tuple-element.125), channel_id=1, source_target_pairs={{0,2},{1,3},{4,6},{5,7}} | collective-permute-start | bytes 62216 | tf_op jit(solution)/shard_map/ppermute | solution.py:19
  61.8 33.2 %collective-permute-start.2 = (f32[1,72,72]{2,0,1:T(1,128)}, f32[1,72,72]{2,0,1:T(1,128)S(1)}, u32[]{:S(2)}, u32[]{:S(2)}) collective-permute-start(f32[1,72,72]{2,0,1:T(1,128)} %bitcast.66), channel_id=1, source_target_pairs={{1,0},{3,2},{5,4},{7,6}} | collective-permute-start | bytes 62216 | tf_op jit(solution)/shard_map/ppermute | solution.py:20
  68.8 26.1 %collective-permute-start.3 = (f32[1,72,72]{2,0,1:T(1,128)S(1)}, f32[1,72,72]{2,0,1:T(1,128)S(1)}, u32[]{:S(2)}, u32[]{:S(2)}) collective-permute-start(f32[1,72,72]{2,0,1:T(1,128)S(1)} %bitcast.65), channel_id=1, source_target_pairs={{0,1},{2,3},{4,5},{6,7}} | collective-permute-start | bytes 62216 | tf_op jit(solution)/shard_map/ppermute | solution.py:19
  75.1 19.8 %collective-permute-start.1 = (f32[1,72,72]{2,0,1:T(1,128)S(1)}, f32[1,72,72]{2,0,1:T(1,128)S(1)}, u32[]{:S(2)}, u32[]{:S(2)}) collective-permute-start(f32[1,72,72]{2,0,1:T(1,128)S(1)} %bitcast.68), channel_id=1, source_target_pairs={{1,0},{3,2},{5,4},{7,6}} | collective-permute-start | bytes 62216 | tf_op jit(solution)/shard_map/ppermute | solution.py:20
  117.4 16.7 %collective-permute-start.16 = (f32[72,72,1]{1,0,2:T(8,128)S(1)}, f32[72,72,1]{1,0,2:T(8,128)S(1)}, u32[]{:S(2)}, u32[]{:S(2)}) collective-permute-start(f32[72,72,1]{1,0,2:T(8,128)S(1)} %copy.106), channel_id=1, source_target_pairs={{4,0},{5,1},{6,2},{7,3}} | collective-permute-start | bytes 62216 | tf_op jit(solution)/shard_map/ppermute | solution.py:20
  121.3 18.6 %collective-permute-start.17 = (f32[72,72,1]{1,0,2:T(8,128)S(1)}, f32[72,72,1]{1,0,2:T(8,128)S(1)}, u32[]{:S(2)}, u32[]{:S(2)}) collective-permute-start(f32[72,72,1]{1,0,2:T(8,128)S(1)} %copy.108), channel_id=1, source_target_pairs={{0,4},{1,5},{2,6},{3,7}} | collective-permute-start | bytes 62216 | tf_op jit(solution)/shard_map/ppermute | solution.py:19
  125.8 16.4 %collective-permute-start.14 = (f32[72,1,72]{2,0,1:T(8,128)S(1)}, f32[72,1,72]{2,0,1:T(8,128)S(1)}, u32[]{:S(2)}, u32[]{:S(2)}) collective-permute-start(f32[72,1,72]{2,0,1:T(8,128)S(1)} %get-tuple-element.116), channel_id=1, source_target_pairs={{2,0},{3,1},{6,4},{7,5}} | collective-permute-start | bytes 62216 | tf_op jit(solution)/shard_map/ppermute | solution.py:20
  132.8 18.5 %collective-permute-start.12 = (f32[1,72,72]{2,0,1:T(1,128)S(1)}, f32[1,72,72]{2,0,1:T(1,128)S(1)}, u32[]{:S(2)}, u32[]{:S(2)}) collective-permute-start(f32[1,72,72]{2,0,1:T(1,128)S(1)} %get-tuple-element.114), channel_id=1, source_target_pairs={{1,0},{3,2},{5,4},{7,6}} | collective-permute-start | bytes 62216 | tf_op jit(solution)/shard_map/ppermute | solution.py:20
  134.1 17.2 %collective-permute-start.13 = (f32[1,72,72]{2,0,1:T(1,128)S(1)}, f32[1,72,72]{2,0,1:T(1,128)S(1)}, u32[]{:S(2)}, u32[]{:S(2)}) collective-permute-start(f32[1,72,72]{2,0,1:T(1,128)S(1)} %get-tuple-element.113), channel_id=1, source_target_pairs={{0,1},{2,3},{4,5},{6,7}} | collective-permute-start | bytes 62216 | tf_op jit(solution)/shard_map/ppermute | solution.py:19
  225.4 17.6 %collective-permute-start.23 = (f32[72,72,1]{1,0,2:T(8,128)S(1)}, f32[72,72,1]{1,0,2:T(8,128)S(1)}, u32[]{:S(2)}, u32[]{:S(2)}) collective-permute-start(f32[72,72,1]{1,0,2:T(8,128)S(1)} %copy.113), channel_id=1, source_target_pairs={{0,4},{1,5},{2,6},{3,7}} | collective-permute-start | bytes 62216 | tf_op jit(solution)/shard_map/ppermute | solution.py:19
  235.9 16.3 %collective-permute-start.18 = (f32[1,72,72]{2,0,1:T(1,128)S(1)}, f32[1,72,72]{2,0,1:T(1,128)S(1)}, u32[]{:S(2)}, u32[]{:S(2)}) collective-permute-start(f32[1,72,72]{2,0,1:T(1,128)S(1)} %get-tuple-element.108), channel_id=1, source_target_pairs={{1,0},{3,2},{5,4},{7,6}} | collective-permute-start | bytes 62216 | tf_op jit(solution)/shard_map/ppermute | solution.py:20
  328.8 17.4 %collective-permute-start.29 = (f32[72,72,1]{1,0,2:T(8,128)S(1)}, f32[72,72,1]{1,0,2:T(8,128)S(1)}, u32[]{:S(2)}, u32[]{:S(2)}) collective-permute-start(f32[72,72,1]{1,0,2:T(8,128)S(1)} %copy.117), channel_id=1, source_target_pairs={{0,4},{1,5},{2,6},{3,7}} | collective-permute-start | bytes 62216 | tf_op jit(solution)/shard_map/ppermute | solution.py:19
  431.7 17.4 %collective-permute-start.35 = (f32[72,72,1]{1,0,2:T(8,128)S(1)}, f32[72,72,1]{1,0,2:T(8,128)S(1)}, u32[]{:S(2)}, u32[]{:S(2)}) collective-permute-start(f32[72,72,1]{1,0,2:T(8,128)S(1)} %copy.121), channel_id=1, source_target_pairs={{0,4},{1,5},{2,6},{3,7}} | collective-permute-start | bytes 62216 | tf_op jit(solution)/shard_map/ppermute | solution.py:19
  442.2 16.1 %collective-permute-start.30 = (f32[1,72,72]{2,0,1:T(1,128)S(1)}, f32[1,72,72]{2,0,1:T(1,128)S(1)}, u32[]{:S(2)}, u32[]{:S(2)}) collective-permute-start(f32[1,72,72]{2,0,1:T(1,128)S(1)} %get-tuple-element.96), channel_id=1, source_target_pairs={{1,0},{3,2},{5,4},{7,6}} | collective-permute-start | bytes 62216 | tf_op jit(solution)/shard_map/ppermute | solution.py:20
  534.8 17.6 %collective-permute-start.41 = (f32[72,72,1]{1,0,2:T(8,128)S(1)}, f32[72,72,1]{1,0,2:T(8,128)S(1)}, u32[]{:S(2)}, u32[]{:S(2)}) collective-permute-start(f32[72,72,1]{1,0,2:T(8,128)S(1)} %copy.125), channel_id=1, source_target_pairs={{0,4},{1,5},{2,6},{3,7}} | collective-permute-start | bytes 62216 | tf_op jit(solution)/shard_map/ppermute | solution.py:19
  545.3 16.3 %collective-permute-start.36 = (f32[1,72,72]{2,0,1:T(1,128)S(1)}, f32[1,72,72]{2,0,1:T(1,128)S(1)}, u32[]{:S(2)}, u32[]{:S(2)}) collective-permute-start(f32[1,72,72]{2,0,1:T(1,128)S(1)} %get-tuple-element.90), channel_id=1, source_target_pairs={{1,0},{3,2},{5,4},{7,6}} | collective-permute-start | bytes 62216 | tf_op jit(solution)/shard_map/ppermute | solution.py:20
  637.8 17.4 %collective-permute-start.47 = (f32[72,72,1]{1,0,2:T(8,128)S(1)}, f32[72,72,1]{1,0,2:T(8,128)S(1)}, u32[]{:S(2)}, u32[]{:S(2)}) collective-permute-start(f32[72,72,1]{1,0,2:T(8,128)S(1)} %copy.129), channel_id=1, source_target_pairs={{0,4},{1,5},{2,6},{3,7}} | collective-permute-start | bytes 62216 | tf_op jit(solution)/shard_map/ppermute | solution.py:19
  740.5 17.5 %collective-permute-start.53 = (f32[72,72,1]{1,0,2:T(8,128)S(1)}, f32[72,72,1]{1,0,2:T(8,128)S(1)}, u32[]{:S(2)}, u32[]{:S(2)}) collective-permute-start(f32[72,72,1]{1,0,2:T(8,128)S(1)} %copy.133), channel_id=1, source_target_pairs={{0,4},{1,5},{2,6},{3,7}} | collective-permute-start | bytes 62216 | tf_op jit(solution)/shard_map/ppermute | solution.py:19
  843.3 17.4 %collective-permute-start.59 = (f32[72,72,1]{1,0,2:T(8,128)S(1)}, f32[72,72,1]{1,0,2:T(8,128)S(1)}, u32[]{:S(2)}, u32[]{:S(2)}) collective-permute-start(f32[72,72,1]{1,0,2:T(8,128)S(1)} %copy.137), channel_id=1, source_target_pairs={{0,4},{1,5},{2,6},{3,7}} | collective-permute-start | bytes 62216 | tf_op jit(solution)/shard_map/ppermute | solution.py:19
  (81 other events, 1078.0 us)
where the time goes:
time: 965 us; the launch traced here: 955 us
  blocking collectives  361 us (37%)
  other arithmetic  234 us (24%)
  local copies, waits for them, and re-layouts  169 us (18%)
  starting transfers between devices  164 us (17%)
  between operations  22.2 us (2%)
    psum x16, blocking collectives, global_sum(): return lax.psum(local_value, MESH_AXES)  361 us
    ppermute x30, starting transfers between devices, neighbour_layers(): from_below = lax.ppermute(top_layer, GRID_AXES[axis_dim], upward)  125 us
    mul x27, other arithmetic, apply_operator(): face_coefs[axis_dim]  98.9 us
    slice x38, local copies, waits for them, and re-layouts, neighbour_layers(): lax.slice_in_dim(grid_field, size_here - 1, size_here, axis=axis_dim)  60.3 us
    reduce_sum x8, other arithmetic, local_solve(): jnp.sum(residual * precond)  52.5 us
    ppermute x30, starting transfers between devices, neighbour_layers(): from_above = lax.ppermute(low_layer, GRID_AXES[axis_dim], downward)  38.7 us
    reduce_sum x8, other arithmetic, local_solve(): step_alpha = rz_old / global_sum(jnp.sum(direction * q_vec))  29.9 us
    unnamed x98, local copies, waits for them, and re-layouts  24.6 us
  transfers between devices with their start and end apart: 60, of which 2 were waited for; matrix products, arithmetic and copies ran while one was open for 17% of the time, Pallas kernels for 0%

commit v1 on v0

v1 whole, which is shorter than its diff:
```python
import functools

import jax
import jax.numpy as jnp
from jax import lax
from jax.experimental import pallas as pl
from jax.experimental.pallas import tpu as pltpu
from jax.sharding import PartitionSpec as P


N = 72
H = 8
E = N + H
NB = 10
STEPS = 8
MESH = pl.DeviceIdType.MESH
F32 = jnp.float32
OTHERS = [(fx, fy, fz) for fx in (0, 1) for fy in (0, 1) for fz in (0, 1) if fx or fy or fz]
NDOT = 24
SUB = 8
LANES = 128
TILES = 9
PART = 24


def iota(axis):
    return lax.broadcasted_iota(jnp.int32, (SUB, LANES), axis)


def two_sum(a, b):
    s = a + b
    t = s - a
    return s, (a - (s - t)) + (b - t)


def quick(a, b):
    s = a + b
    return s, b - (s - a)


def two_prod(a, b):
    def split(x):
        t = x * 4097.0
        hi = t - (t - x)
        return hi, x - hi
    p = a * b
    ah, al = split(a)
    bh, bl = split(b)
    return p, ((ah * bh - p) + ah * bl + al * bh) + al * bl


def dadd(x, y):
    (xh, xl), (yh, yl) = x, y
    s, e = two_sum(xh, yh)
    return quick(s, e + (xl + yl))


def dsub(x, y):
    yh, yl = y
    return dadd(x, (-yh, -yl))


def dscale(x, c):
    hi, lo = x
    return hi * c, lo * c


def dmul(x, y):
    (xh, xl), (yh, yl) = x, y
    p, e = two_prod(xh, yh)
    return quick(p, e + (xh * yl + xl * yh))


def ddiv(x, y):
    (xh, xl), (yh, yl) = x, y
    q = xh / yh
    p, e = two_prod(q, yh)
    rest = ((xh - p) - e) + (xl - q * yl)
    return quick(q, rest / yh)


def step_lengths(m):
    alphas, betas = [], []
    y = dict(enumerate(m))
    p = {0: dsub(y[0], y[1])}
    for l in range(1, 15):
        p[l] = dsub(y[l], dscale(dadd(y[l + 1], y[l - 1]), 0.5))
    for t in range(STEPS):
        alpha = ddiv(y[t], p[t])
        alphas.append(alpha[0])
        if t == STEPS - 1:
            break
        y_next = {l: dsub(y[l], dmul(alpha, p[l])) for l in range(t + 1, 15 - t)}
        beta = ddiv(y_next[t + 1], p[t])
        if t:
            beta = dscale(beta, 0.5)
        betas.append(beta[0])
        p_next = {}
        for l in range(t + 1, 14 - t):
            side = y_next[l + 1] if l == t + 1 else dadd(y_next[l + 1], y_next[l - 1])
            p_next[l] = dadd(dsub(y_next[l], dscale(side, 0.5)), dmul(beta, p[l]))
        y, p = y_next, p_next
    return alphas, betas


def basis_coefs(alphas, betas):
    def add(a, b):
        return b if a is None else (a if b is None else a + b)

    def axpy(x, c, y):
        return [xi if yi is None else (c * yi if xi is None else xi + c * yi) for xi, yi in zip(x, y)]

    def apply_op(v):
        out = [None] * 11
        out[1] = v[0]
        for j in range(SUB):
            if v[1 + j] is None:
                continue
            c = v[1 + j]
            out[1 + j] = add(out[1 + j], c)
            if j == 0:
                out[2] = add(out[2], -c)
            else:
                half = -0.5 * c
                out[2 + j] = add(out[2 + j], half)
                out[j] = add(out[j], half)
        return out[:TILES]

    one = jnp.ones_like(alphas[0])
    y = [one] + [None] * SUB
    p = list(y)
    x = [None] * TILES
    ys = []
    for t in range(STEPS):
        q = apply_op(p)
        x = axpy(x, alphas[t], p)
        y = axpy(y, -alphas[t], q)
        ys.append(y)
        if t < STEPS - 1:
            p = axpy(y, betas[t], p)
    return ys, x


def row_down(v):
    return jnp.concatenate([pltpu.roll(v[NB - 1], 1, 0)[None], v[:NB - 1]], axis=0)


def row_up(v):
    return jnp.concatenate([v[1:], pltpu.roll(v[0], 7, 0)[None]], axis=0)


def lane_down(v):
    return pltpu.roll(v, 1, 2)


def lane_up(v):
    return pltpu.roll(v, 127, 2)


def load_chunk(ref, plane):
    return jnp.stack([ref[plane, pl.ds(b, SUB, stride=NB), :] for b in range(NB)], axis=0)


def replace(v, b, mask, value):
    return jnp.concatenate(([v[:b]] if b else []) + [jnp.where(mask, value, v[b])[None], v[b + 1:]], axis=0)


def harmonic(a, b):
    return 2.0 * a * b / (a + b)


def dot_pair(a, b):
    prod = a * b
    return jnp.sum(prod[:2], axis=0), jnp.sum(prod[2:], axis=0)


def own_cells(low, high):
    sub, lane = iota(0), iota(1)
    return jnp.where(lane < N, low + jnp.where(sub < 7, high, 0.0), 0.0)


def kernel(k_hbm, f_hbm, u_hbm, kg_hbm, kgt_hbm, uo_hbm, ro_hbm, rr_ref,
           k_in, u_in, f_in, k_nat, u_nat, z_nat, cx_a, cy_a, cz_a, isd_a, sd_a, v0_a, b_a,
           walls, wz_t, wy, ky, ux, zs, zr, ds_, dr, us, ur, uzs, uzr, acc, gath, rsend, rgath, coef,
           load_sem, out_sem, send_sem, recv_sem, all_send, all_recv):
    cx, cy, cz = lax.axis_index('gx'), lax.axis_index('gy'), lax.axis_index('gz')
    me = cx + 2 * cy + 4 * cz
    lane, sub = iota(1), iota(0)

    def peer(fx, fy, fz):
        out = {}
        if fx:
            out['gx'] = 1 - cx
        if fy:
            out['gy'] = 1 - cy
        if fz:
            out['gz'] = 1 - cz
        return out

    loads = []
    for n, (src, dst) in enumerate([(k_hbm, k_in), (u_hbm, u_in), (f_hbm, f_in)]):
        loads.append(pltpu.make_async_copy(src, dst, load_sem.at[n]))
    loads.append(pltpu.make_async_copy(kg_hbm.at[cx], walls.at[0], load_sem.at[3]))
    loads.append(pltpu.make_async_copy(kg_hbm.at[2 + cy], walls.at[1], load_sem.at[4]))
    loads.append(pltpu.make_async_copy(kgt_hbm.at[cz], walls.at[2], load_sem.at[5]))
    for n in (0, 1, 3, 4, 5, 2):
        loads[n].start()

    barrier = pltpu.get_barrier_semaphore()
    for flips in OTHERS:
        pl.semaphore_signal(barrier, inc=1, device_id=peer(*flips), device_id_type=MESH)
    pl.semaphore_wait(barrier, len(OTHERS))

    def send(n, src, dst, flips):
        copy = pltpu.make_async_remote_copy(src_ref=src, dst_ref=dst, send_sem=send_sem.at[n], recv_sem=recv_sem.at[n],
                                            device_id=peer(*flips), device_id_type=MESH)
        copy.start()
        return copy

    near_y = pl.multiple_of((N - H) * (1 - cy), SUB)
    near_x = (N - H) * (1 - cx)
    group8 = lane // SUB
    src8 = (N - H) * (1 - cz)
    dst8 = N + 48 * cz
    ghost8 = jnp.logical_and(lane >= dst8, lane < dst8 + SUB)
    wall_lane = 127 - 55 * cz
    own_lane = lane < N

    def widen(x):
        return x if x.shape[1] == LANES else jnp.concatenate([x, jnp.zeros((x.shape[0], LANES - x.shape[1]), F32)], axis=1)

    def pack(nat, packed, corner):
        def body(o, carry):
            for q in range(5):
                out = None
                for g in range(min(16, N - 16 * q)):
                    t = 16 * q + g
                    x = widen(nat[o * SUB + t // TILES, pl.ds(SUB * (t % TILES), SUB), :])
                    x = pltpu.roll(x, (SUB * g - src8 + LANES) % LANES, 1)
                    out = x if g == 0 else jnp.where(group8 == g, x, out)
                packed[o * 5 + q] = out
            out = None
            for g in range(SUB):
                x = widen(nat[o * SUB + g, pl.ds(near_y, SUB), :])
                x = pltpu.roll(x, (SUB * g - src8 + LANES) % LANES, 1)
                out = x if g == 0 else jnp.where(group8 == g, x, out)
            corner[o] = out
            return carry
        lax.fori_loop(0, TILES, body, 0)

    def unpack(own, side, nat, packed, corner, fill, wall):
        def body(o, carry):
            for pi in range(SUB):
                i = o * SUB + pi
                for jt in range(10):
                    if jt < TILES:
                        t = pi * TILES + jt
                        got, g = packed[o * 5 + t // 16], t % 16
                    else:
                        got, g = corner[o], pi
                    got = pltpu.roll(got, (dst8 - SUB * g + LANES) % LANES, 1)
                    x = widen(own[i, pl.ds(SUB * jt, SUB), :] if jt < TILES else side[i])
                    x = jnp.where(own_lane, x, jnp.where(ghost8, got, fill))
                    if wall is not None:
                        w = pltpu.roll(wall[pl.ds(SUB * jt, SUB), :], (wall_lane - i + LANES) % LANES, 1)
                        x = jnp.where(lane == wall_lane, w, x)
                    nat[i, pl.ds(SUB * jt, SUB), :] = x
            return carry
        lax.fori_loop(0, TILES, body, 0)

    loads[0].wait()
    k_y = send(0, k_in.at[:, pl.ds(near_y, SUB), :], ky, (0, 1, 0))
    pack(k_in, zs.at[0], ds_.at[0])
    loads[1].wait()
    u_row = (N - 1) * (1 - cy)
    u_lane = (N - 1) * (1 - cz)
    u_x = send(5, u_in.at[pl.ds((N - 1) * (1 - cx), 1)], ux, (1, 0, 0))

    def pack_u(o, carry):
        us[pl.ds(pl.multiple_of(o * SUB, SUB), SUB), :] = jnp.concatenate(
            [u_in[o * SUB + r, pl.ds(u_row, 1), :] for r in range(SUB)], axis=0)
        out = None
        for t in range(N):
            x = widen(u_in[o * SUB + t // TILES, pl.ds(SUB * (t % TILES), SUB), :])
            x = pltpu.roll(x, (t - u_lane + LANES) % LANES, 1)
            out = x if t == 0 else jnp.where(lane == t, x, out)
        uzs[o] = out
        return carry
    lax.fori_loop(0, TILES, pack_u, 0)

    k_z = send(1, zs.at[0], zr.at[0], (0, 0, 1))
    k_d = send(2, ds_.at[0], dr.at[0], (0, 1, 1))
    u_y = send(3, us, ur, (0, 1, 0))
    u_z = send(4, uzs, uzr, (0, 0, 1))

    for n in (3, 4, 5):
        loads[n].wait()

    def lane_ring(w, at, c):
        left, right = walls[w, pl.ds(at, SUB), 0:LANES], walls[w, pl.ds(at, SUB), LANES:144]
        right = jnp.concatenate([jnp.zeros((SUB, 56), F32), right, jnp.zeros((SUB, 56), F32)], axis=1)
        turned = jnp.where(jnp.logical_and(lane >= 56, lane < N), right, pltpu.roll(left, 56, 1))
        return jnp.where(c == 0, left, turned)

    for jt in range(10):
        at_j = pl.multiple_of(N * cy + SUB * jt if jt < TILES else N - H * cy, SUB)
        at_i = pl.multiple_of(N * cx + SUB * jt if jt < TILES else N - H * cx, SUB)
        k_nat[E, pl.ds(SUB * jt, SUB), :] = lane_ring(0, at_j, cz)
        wy[pl.ds(SUB * jt, SUB), :] = lane_ring(1, at_i, cz)
        wz_t[pl.ds(SUB * jt, SUB), :] = lane_ring(2, at_j, cx)

    loads[2].wait()

    def take_f(p, carry):
        for b in range(NB):
            rows = SUB if b < 2 else 7
            v0_a[p, b, 0:rows, 0:N] = f_in[p, pl.ds(b, rows, stride=NB), :]
        return carry
    lax.fori_loop(0, N, take_f, 0)

    k_y.wait()
    k_z.wait()
    k_d.wait()
    unpack(k_in, ky, k_nat, zr.at[0], dr.at[0], 1.0, wz_t)
    k_x = send(6, k_nat.at[pl.ds(near_x, SUB)], k_nat.at[pl.ds(N, SUB)], (1, 0, 0))

    u_z.wait()
    u_dst = N + 55 * cz

    def unpack_u(o, carry):
        for t in range(N):
            i, j = o * SUB + t // TILES, SUB * (t % TILES)
            got = pltpu.roll(uzr[o], (u_dst - t + LANES) % LANES, 1)
            x = widen(u_in[i, pl.ds(j, SUB), :])
            u_nat[i, pl.ds(j, SUB), :] = jnp.where(own_lane, x, jnp.where(lane == u_dst, got, 0.0))
        return carry
    u_x.wait()
    lax.fori_loop(0, TILES, unpack_u, 0)
    u_nat[E - 1 - 7 * cx] = jnp.zeros((E, LANES), F32)
    u_nat[N + 7 * cx, 0:N, 0:N] = ux[0]
    u_y.wait()
    k_x.wait()

    row0 = sub == 0
    row72 = sub == 7

    def faces(p, carry):
        kc = load_chunk(k_nat, p)
        before = jnp.where(jnp.logical_and(p == 0, cx == 0), E, jnp.where(p == 0, E - 1, p - 1))
        here = jnp.where(jnp.logical_and(p == N, cx == 1), E, p)
        cx_a[p] = harmonic(load_chunk(k_nat, here), load_chunk(k_nat, before))
        wall = jnp.broadcast_to(wy[pl.ds(p, 1), :], (SUB, LANES))
        low = replace(row_down(kc), 0, jnp.logical_and(row0, cy == 0), wall)
        high = replace(kc, 2, jnp.logical_and(row72, cy == 1), wall)
        cy_a[p] = harmonic(high, low)
        cz_a[p] = harmonic(kc, lane_down(kc))
        return carry
    lax.fori_loop(0, E, faces, 0)
    cx_a[E] = cx_a[0]

    def divergence(h_x, h_xn, h_y, h_z, v, v_prev, v_next, low_row, high_row):
        low = row_down(v)
        high = v
        if low_row is not None:
            low = replace(low, 0, row0, low_row)
            high = replace(v, 2, row72, high_row)
        else:
            low = replace(low, 0, jnp.logical_and(row0, cy == 0), 0.0)
            high = replace(v, 2, jnp.logical_and(row72, cy == 1), 0.0)
        f_y = h_y * (high - low)
        f_z = h_z * (v - lane_down(v))
        return ((h_x * (v - v_prev) - h_xn * (v_next - v)) + (f_y - row_up(f_y))) + (f_z - lane_up(f_z))

    def diag_of(p):
        h_x, h_xn, h_y, h_z = cx_a[p], cx_a[p + 1], cy_a[p], cz_a[p]
        d = ((h_x + h_xn) + (h_y + row_up(h_y))) + (h_z + lane_up(h_z))
        inv = lax.rsqrt(d)
        isd_a[p] = inv
        return h_x, h_xn, h_y, h_z, inv, d

    def start_own(p, carry):
        h_x, h_xn, h_y, h_z, inv, d = diag_of(p)
        sd_a[p] = d * inv
        before = jnp.where(p == 0, E - 1, p - 1)
        got = jnp.broadcast_to(widen(ur[pl.ds(p, 1), :]), (SUB, LANES))
        low_row = jnp.where(cy == 0, 0.0, got)
        high_row = jnp.where(cy == 0, got, 0.0)
        a_u = divergence(h_x, h_xn, h_y, h_z, load_chunk(u_nat, p), load_chunk(u_nat, before), load_chunk(u_nat, p + 1),
                         low_row, high_row)
        y0 = (v0_a[p] - a_u) * inv
        v0_a[p] = y0
        z0 = y0 * inv
        for b in range(NB):
            if b < 2:
                z_nat[p, pl.ds(b, SUB, stride=NB), :] = z0[b]
            else:
                z_nat[p, pl.ds(b, 7, stride=NB), :] = z0[b, :7]
        return carry
    lax.fori_loop(0, N, start_own, 0)

    def start_ghost(p, carry):
        diag_of(p)
        return carry

    z_y = send(7, z_nat.at[pl.ds(0, N), pl.ds(near_y, SUB), :], z_nat.at[pl.ds(0, N), pl.ds(N, SUB), :], (0, 1, 0))
    pack(z_nat, zs.at[1], ds_.at[1])
    lax.fori_loop(N, E, start_ghost, 0)
    z_z = send(SUB, zs.at[1], zr.at[1], (0, 0, 1))
    z_d = send(TILES, ds_.at[1], dr.at[1], (0, 1, 1))
    z_y.wait()
    z_z.wait()
    z_d.wait()
    unpack(z_nat, z_nat.at[:, pl.ds(N, SUB), :], z_nat, zr.at[1], dr.at[1], 0.0, None)
    z_x = send(10, z_nat.at[pl.ds(near_x, SUB)], z_nat.at[pl.ds(N, SUB)], (1, 0, 0))
    z_x.wait()

    def first(own, p, carry):
        before = jnp.where(p == 0, E - 1, p - 1)
        after = jnp.where(p == E - 1, 0, p + 1)
        h_x, h_xn, h_y, h_z, inv = cx_a[p], cx_a[p + 1], cy_a[p], cz_a[p], isd_a[p]
        z_p = jnp.where(jnp.logical_and(p == 0, cx == 0), 0.0, load_chunk(z_nat, before))
        z_n = jnp.where(jnp.logical_and(p == N - 1, cx == 1), 0.0, load_chunk(z_nat, after))
        b0 = inv * divergence(h_x, h_xn, h_y, h_z, load_chunk(z_nat, p), z_p, z_n, None, None)
        b_a[0, p] = b0
        cut = jnp.logical_or(jnp.logical_and(p == 0, cx == 0), jnp.logical_and(p == N, cx == 1))
        twice = 2.0 * inv
        cx_a[p] = jnp.where(cut, 0.0, h_x * (twice * isd_a[before]))
        c_y = h_y * (twice * row_down(inv))
        c_y = replace(c_y, 0, jnp.logical_and(row0, cy == 0), 0.0)
        cy_a[p] = replace(c_y, 2, jnp.logical_and(row72, cy == 1), 0.0)
        c_z = h_z * (twice * lane_down(inv))
        edge = N * cz
        cz_a[p] = jnp.where(lax.broadcasted_iota(jnp.int32, (NB, SUB, LANES), 2) == edge, 0.0, c_z)
        if not own:
            return carry
        v0 = v0_a[p]
        new = dot_pair(v0, v0) + dot_pair(v0, b0) + dot_pair(b0, b0)
        return tuple(c + n for c, n in zip(carry, new))

    zero = jnp.zeros((SUB, LANES), F32)
    sums = lax.fori_loop(0, N, functools.partial(first, True), (zero,) * 6)
    lax.fori_loop(N, E, functools.partial(first, False), 0)
    cx_a[E] = cx_a[0]
    acc[0] = own_cells(sums[0], sums[1])
    acc[1] = own_cells(sums[2], sums[3])
    acc[TILES] = own_cells(sums[4], sums[5])
    acc[23] = zero

    def advance(k, own, p, carry):
        before = jnp.where(p == 0, E - 1, p - 1)
        after = jnp.where(p == E - 1, 0, p + 1)
        v = b_a[k - 1, p]
        c_y, c_z = cy_a[p], cz_a[p]
        new = cx_a[p] * b_a[k - 1, before] + cx_a[p + 1] * b_a[k - 1, after]
        new = new + (c_y * row_down(v) + row_up(c_y * v))
        new = new + (c_z * lane_down(v) + lane_up(c_z * v))
        new = 0.5 * new if k == 1 else new - b_a[k - 2, p]
        b_a[k, p] = new
        if not own:
            return carry
        dots = dot_pair(v0_a[p], new) + dot_pair(v, new) + dot_pair(new, new)
        return tuple(c + n for c, n in zip(carry, dots))

    for k in range(1, STEPS):
        sums = lax.fori_loop(0, N, functools.partial(advance, k, True), (zero,) * 6)
        if k < STEPS - 1:
            lax.fori_loop(N, E, functools.partial(advance, k, False), 0)
        acc[1 + k] = own_cells(sums[0], sums[1])
        acc[16 + k - 1] = own_cells(sums[2], sums[3])
        if k < STEPS - 1:
            acc[TILES + k] = own_cells(sums[4], sums[5])

    def gather(buf, n_sem):
        copies = []
        for n, flips in enumerate(OTHERS):
            copies.append(pltpu.make_async_remote_copy(
                src_ref=buf.at[me], dst_ref=buf.at[me], send_sem=all_send.at[n_sem, n], recv_sem=all_recv.at[n_sem, n],
                device_id=peer(*flips), device_id_type=MESH))
        for copy in copies:
            copy.start()
        return copies

    hi = acc[:, 0, :]
    lo = jnp.zeros((NDOT, LANES), F32)
    for s in range(1, SUB):
        hi, err = two_sum(hi, acc[:, s, :])
        lo = lo + err
    gath[me, 0:NDOT] = hi
    gath[me, NDOT:2 * NDOT] = lo
    for copy in gather(gath, 0):
        copy.wait()
    hi, lo = gath[0, 0:NDOT], gath[0, NDOT:2 * NDOT]
    for dev in range(1, SUB):
        hi, err = two_sum(hi, gath[dev, 0:NDOT])
        lo = lo + (gath[dev, NDOT:2 * NDOT] + err)
    for shift in (64, 32, 16, SUB, 4, 2, 1):
        hi, err = two_sum(hi, pltpu.roll(hi, shift, 1))
        lo = (lo + pltpu.roll(lo, shift, 1)) + err
    hi, lo = quick(hi, lo)
    size = hi[0:1]
    factor = jnp.where(size > 1e30, 2.0 ** -110, jnp.where(size > 1e12, 2.0 ** -60, jnp.where(
        size < 1e-30, 2.0 ** 110, jnp.where(size < 1e-12, 2.0 ** 60, 1.0)))).astype(F32)
    hi, lo = hi * factor, lo * factor

    def total(row):
        return jnp.broadcast_to(hi[row:row + 1], (SUB, LANES)), jnp.broadcast_to(lo[row:row + 1], (SUB, LANES))

    n_mom = [total(TILES), total(16)]
    for j in range(1, 7):
        n_mom.append(dsub(dscale(total(TILES + j), 2.0), n_mom[0]))
        n_mom.append(dsub(dscale(total(16 + j), 2.0), n_mom[1]))
    l_mom = [total(1 + j) for j in range(SUB)]
    for j in range(7, 14):
        l_mom.append(dsub(dscale(dsub(l_mom[j], n_mom[j]), 2.0), l_mom[j - 1]))
    m_mom = [total(0)]
    m_mom.append(dsub(m_mom[0], l_mom[0]))
    for j in range(1, 15):
        m_mom.append(dsub(dscale(dsub(m_mom[j], l_mom[j]), 2.0), m_mom[j - 1]))
    ys, xs = basis_coefs(*step_lengths(m_mom))
    slot = {}
    for t in range(STEPS):
        for j in range(t + 1):
            slot[t, j] = len(slot)
            coef[slot[t, j]] = ys[t][1 + j]
    for j in range(SUB):
        slot['x', j] = len(slot)
        coef[slot['x', j]] = xs[j]

    def put(ref, p, b0, val):
        for b in range(val.shape[0]):
            if b0 + b < 2:
                ref[p, pl.ds(b0 + b, SUB, stride=NB), :] = val[b, :, :N]
            else:
                ref[p, pl.ds(b0 + b, 7, stride=NB), :] = val[b, :7, :N]

    def residuals(p, carry):
        carry = list(carry)
        for b0 in range(0, NB, 2):
            cut = pl.ds(b0, 2)
            v0, sd = v0_a[p, cut], sd_a[p, cut]
            bs = [b_a[j, p, cut] for j in range(SUB)]
            for t in range(STEPS):
                y = v0
                for j in range(t + 1):
                    y = y + coef[slot[t, j]] * bs[j]
                r = sd * y
                which = 2 * t + (b0 > 0)
                carry[which] = carry[which] + jnp.sum(r * r, axis=0)
                if t == STEPS - 1:
                    put(f_in, p, b0, r)
        return tuple(carry)

    outs = []

    def flush(n, nat, hbm, o):
        outs.append(pltpu.make_async_copy(nat.at[pl.ds(PART * o, PART)], hbm.at[pl.ds(PART * o, PART)],
                                          out_sem.at[n, o]))
        outs[-1].start()

    sums = (zero,) * 16
    for o in range(3):
        sums = lax.fori_loop(PART * o, PART * o + PART, residuals, sums)
        flush(0, f_in, ro_hbm, o)
    for t in range(STEPS):
        rsend[t] = own_cells(sums[2 * t], sums[2 * t + 1])
    part = rsend[:, 0, :]
    for s in range(1, SUB):
        part = part + rsend[:, s, :]
    rgath[me] = part
    rr_copies = gather(rgath, 1)

    def update(p, carry):
        for b0 in range(0, NB, 2):
            cut = pl.ds(b0, 2)
            x = coef[slot['x', 0]] * v0_a[p, cut]
            for j in range(1, SUB):
                x = x + coef[slot['x', j]] * b_a[j - 1, p, cut]
            x = x * isd_a[p, cut]
            u = jnp.stack([u_nat[p, pl.ds(b0 + b, SUB, stride=NB), :] for b in range(2)], axis=0)
            put(k_in, p, b0, u + x)
        return carry

    for o in range(3):
        lax.fori_loop(PART * o, PART * o + PART, update, 0)
        flush(1, k_in, uo_hbm, o)
    for copy in rr_copies:
        copy.wait()
    part = rgath[0]
    for dev in range(1, SUB):
        part = part + rgath[dev]
    part = jnp.broadcast_to(jnp.sum(part, axis=1, keepdims=True), (SUB, LANES))
    rr_ref[...] = part
    for copy in outs:
        copy.wait()


def solution(mesh):
    spec = P('gx', 'gy', 'gz')

    def local(k_cell, k_ghost, f_rhs, u_init):
        kgt = jnp.swapaxes(k_ghost[4:6], 1, 2)
        big = (E, NB, SUB, LANES)
        ext = (E + 1, NB, SUB, LANES)
        vm = lambda *shape: pltpu.VMEM(shape, F32)
        any_spec = pl.BlockSpec(memory_space=pl.ANY)
        block = jax.ShapeDtypeStruct((N, N, N), F32)
        u, r, rr = pl.pallas_call(
            kernel,
            out_shape=(block, block, jax.ShapeDtypeStruct((SUB, LANES), F32)),
            in_specs=[any_spec] * 5,
            out_specs=(any_spec, any_spec, pl.BlockSpec(memory_space=pltpu.VMEM)),
            scratch_shapes=[
                vm(N, N, N), vm(N, N, N), vm(N, N, N), vm(E + 1, E, LANES), vm(E, E, LANES), vm(E, E, LANES),
                vm(*ext), vm(*big), vm(*big), vm(*big), vm(N, NB, SUB, LANES), vm(N, NB, SUB, LANES), vm(SUB, *big),
                vm(3, 144, 144), vm(E, LANES), vm(E, LANES), vm(N, SUB, N), vm(1, N, N),
                vm(2, 45, SUB, LANES), vm(2, 45, SUB, LANES), vm(2, TILES, SUB, LANES), vm(2, TILES, SUB, LANES),
                vm(N, N), vm(N, N), vm(TILES, SUB, LANES), vm(TILES, SUB, LANES),
                vm(NDOT, SUB, LANES), vm(SUB, 2 * NDOT, LANES), vm(SUB, SUB, LANES), vm(SUB, SUB, LANES), vm(44, SUB, LANES),
                pltpu.SemaphoreType.DMA((6,)), pltpu.SemaphoreType.DMA((2, 3)),
                pltpu.SemaphoreType.DMA((11,)), pltpu.SemaphoreType.DMA((11,)),
                pltpu.SemaphoreType.DMA((2, 7)), pltpu.SemaphoreType.DMA((2, 7)),
            ],
            compiler_params=pltpu.CompilerParams(collective_id=0, has_side_effects=True, vmem_limit_bytes=67043328),
        )(k_cell, f_rhs, u_init, k_ghost, kgt)
        return u, r, rr[:, 0]

    return jax.shard_map(local, mesh=mesh, in_specs=(spec, P(), spec, spec), out_specs=(spec, spec, P()), check_vma=False)
```

time: 965 us -> 146 us (0.15); the launches traced: 955 us -> 146 us
  blocking collectives: 361 us -> 0 us
  other arithmetic: 234 us -> 0 us
  starting transfers between devices: 164 us -> 0 us
  local copies, waits for them, and re-layouts: 169 us -> 8.24 us
  Pallas kernels: 0 us -> 137 us
  between operations: 22.2 us -> 0.64 us
    psum x16 -> x0, blocking collectives: 361 us -> none  [global_sum(): return lax.psum(local_value, MESH_AXES)]
    ppermute x60 -> x0, starting transfers between devices: 164 us -> none  [the longest x30 125 us: neighbour_layers(): from_below = lax.ppermute(top_layer, GRID_AXES[axis_dim], upward)]
    pallas_call x0 -> x1, Pallas kernels: none -> 137 us  [local(): pl.pallas_call(kernel, out_shape=(block, block, jax.ShapeDtypeStruct((SUB...]
    mul x28 -> x0, other arithmetic: 112 us -> none  [the longest x27 98.9 us: apply_operator(): face_coefs[axis_dim]]
    slice x55 -> x2, local copies, waits for them, and re-layouts: 87.8 us -> 2.28 us  [the longest x1 1.3 us: local(): return (u, r, rr[:, 0])]
    reduce_sum x16 -> x0, other arithmetic: 82.3 us -> none  [the longest x8 52.5 us: local_solve(): jnp.sum(residual * precond)]
    ppermute x18 -> x0, local copies, waits for them, and re-layouts: 44.3 us -> none  [the longest x9 22.3 us: neighbour_layers(): from_above = lax.ppermute(low_layer, GRID_AXES[axis_dim], downward)]
    add x8 -> x0, other arithmetic: 25 us -> none  [the longest x7 14.9 us: local_solve(): direction = precond + pair_sums[0] / rz_old * direction]
  transfers between devices with their start and end apart: 60 -> 0, of which waited for: 2 -> 0; matrix products, arithmetic and copies ran while one was open for 17% -> 0% of each run, Pallas kernels for 0% -> 0%
where the time goes in v1:
time: 146 us
  Pallas kernels  137 us (94%)
  local copies, waits for them, and re-layouts  8.24 us (6%)
    pallas_call x1, Pallas kernels, local(): pl.pallas_call(kernel, out_shape=(block, block, jax.ShapeDtypeStruct((SUB...  137 us
    unnamed x5, local copies, waits for them, and re-layouts  5.96 us

profile of v1, /device:TPU:0, one launch (start us, length us, event | category | flops | bytes accessed | tf_op | source)
XLA Modules:
  0.0 145.7 jit_solution(2834330097095801576)
XLA Ops:
  0.6 1.0 slice.6
  1.6 0.9 copy.9
  2.5 136.9 %shard_map.67 = (f32[72,72,72]{2,1,0:T(8,128)}, f32[72,72,72]{2,1,0:T(8,128)}, f32[8,128]{1,0:T(8,128)}) custom-call(f32[72,72,72]{2,1,0:T(8,128)} %k_hbm.1, f32[72,72,72]{2,1,0:T(8,128)} %f_hbm.1, f32[72,72,72]{2,1,0:T(8,128)} %u_hbm.1, f32[6,144,144]{2,1,0:T(8,128)} %kg_hbm.1, f32[2,144,144]{2,1,0:T(8,128)} %bitcast.1), custom_call_target="tpu_custom_call" | custom-call | tf_op jit(solution)/shard_map/pallas_call | solution.py:607
  139.4 1.3 slice_reduce_fusion
  140.7 0.0 copy-start
  140.7 3.6 %copy.12 = f32[72,72,72]{2,1,0:T(8,128)} copy(f32[72,72,72]{2,1,0:T(8,128)} %get-tuple-element.12) | data formatting | bytes 2985984
  144.2 0.0 copy-done
  144.2 1.5 %copy.13 = f32[72,72,72]{2,1,0:T(8,128)} copy(f32[72,72,72]{2,1,0:T(8,128)S(1)} %copy-done) | data formatting | bytes 2985984
Async XLA Ops:
  140.7 3.6 %copy-start = (f32[72,72,72]{2,1,0:T(8,128)S(1)}, f32[72,72,72]{2,1,0:T(8,128)}, u32[]{:S(2)}) copy-start(f32[72,72,72]{2,1,0:T(8,128)} %get-tuple-element.13) | copy-start | bytes 4478980

commit v2 on v1

--- a/solution.py
+++ b/solution.py
@@ -174,17 +174,26 @@
     return jnp.sum(prod[:2], axis=0), jnp.sum(prod[2:], axis=0)
 
 
+def planes(lo, hi, body, init, width=4):
+    def some(n, carry):
+        for w in range(width):
+            carry = body(lo + n * width + w, carry)
+        return carry
+    return lax.fori_loop(0, (hi - lo) // width, some, init)
+
+
 def own_cells(low, high):
     sub, lane = iota(0), iota(1)
     return jnp.where(lane < N, low + jnp.where(sub < 7, high, 0.0), 0.0)
 
 
-def kernel(k_hbm, f_hbm, u_hbm, kg_hbm, kgt_hbm, uo_hbm, ro_hbm, rr_ref,
-           k_in, u_in, f_in, k_nat, u_nat, z_nat, cx_a, cy_a, cz_a, isd_a, sd_a, v0_a, b_a,
-           walls, wz_t, wy, ky, ux, zs, zr, ds_, dr, us, ur, uzs, uzr, acc, gath, rsend, rgath, coef,
+def kernel(k_hbm, f_hbm, u_hbm, kg_hbm, uo_hbm, ro_hbm, rr_ref,
+           k_in, u_in, f_in, k_nat, u_nat, z_nat, cx_a, cy_a, cz_a, isd_a, v0_a, b0_a, b1_a, b2_a, b3_a, b4_a, b5_a, b6_a, b7_a,
+           walls, wz, wz_t, wy, ky, ux, zs, zr, ds_, dr, us, ur, uzs, uzr, acc, gath, rsend, rgath, coef,
            load_sem, out_sem, send_sem, recv_sem, all_send, all_recv):
     cx, cy, cz = lax.axis_index('gx'), lax.axis_index('gy'), lax.axis_index('gz')
     me = cx + 2 * cy + 4 * cz
+    b_a = (b0_a, b1_a, b2_a, b3_a, b4_a, b5_a, b6_a, b7_a)
     lane, sub = iota(1), iota(0)
 
     def peer(fx, fy, fz):
@@ -202,7 +211,7 @@
         loads.append(pltpu.make_async_copy(src, dst, load_sem.at[n]))
     loads.append(pltpu.make_async_copy(kg_hbm.at[cx], walls.at[0], load_sem.at[3]))
     loads.append(pltpu.make_async_copy(kg_hbm.at[2 + cy], walls.at[1], load_sem.at[4]))
-    loads.append(pltpu.make_async_copy(kgt_hbm.at[cz], walls.at[2], load_sem.at[5]))
+    loads.append(pltpu.make_async_copy(kg_hbm.at[4 + cz], walls.at[2], load_sem.at[5]))
     for n in (0, 1, 3, 4, 5, 2):
         loads[n].start()
 
@@ -262,7 +271,8 @@
                     x = widen(own[i, pl.ds(SUB * jt, SUB), :] if jt < TILES else side[i])
                     x = jnp.where(own_lane, x, jnp.where(ghost8, got, fill))
                     if wall is not None:
-                        w = pltpu.roll(wall[pl.ds(SUB * jt, SUB), :], (wall_lane - i + LANES) % LANES, 1)
+                        at = SUB * jt if jt < TILES else pl.multiple_of(N + 48 * cy, SUB)
+                        w = pltpu.roll(wall[pl.ds(at, SUB), :], (wall_lane - i + LANES) % LANES, 1)
                         x = jnp.where(lane == wall_lane, w, x)
                     nat[i, pl.ds(SUB * jt, SUB), :] = x
             return carry
@@ -307,7 +317,8 @@
         at_i = pl.multiple_of(N * cx + SUB * jt if jt < TILES else N - H * cx, SUB)
         k_nat[E, pl.ds(SUB * jt, SUB), :] = lane_ring(0, at_j, cz)
         wy[pl.ds(SUB * jt, SUB), :] = lane_ring(1, at_i, cz)
-        wz_t[pl.ds(SUB * jt, SUB), :] = lane_ring(2, at_j, cx)
+        if jt < TILES:
+            wz[pl.ds(SUB * jt, SUB), :] = lane_ring(2, at_i, cy)
 
     loads[2].wait()
 
@@ -317,6 +328,8 @@
             v0_a[p, b, 0:rows, 0:N] = f_in[p, pl.ds(b, rows, stride=NB), :]
         return carry
     lax.fori_loop(0, N, take_f, 0)
+
+    wz_t[...] = wz[...].T
 
     k_y.wait()
     k_z.wait()
@@ -355,7 +368,7 @@
         cy_a[p] = harmonic(high, low)
         cz_a[p] = harmonic(kc, lane_down(kc))
         return carry
-    lax.fori_loop(0, E, faces, 0)
+    planes(0, E, faces, 0)
     cx_a[E] = cx_a[0]
 
     def divergence(h_x, h_xn, h_y, h_z, v, v_prev, v_next, low_row, high_row):
@@ -380,7 +393,9 @@
 
     def start_own(p, carry):
         h_x, h_xn, h_y, h_z, inv, d = diag_of(p)
-        sd_a[p] = d * inv
+        sd = d * inv
+        for b in range(NB):
+            k_nat[p, pl.ds(SUB * b, SUB), :] = sd[b]
         before = jnp.where(p == 0, E - 1, p - 1)
         got = jnp.broadcast_to(widen(ur[pl.ds(p, 1), :]), (SUB, LANES))
         low_row = jnp.where(cy == 0, 0.0, got)
@@ -396,7 +411,7 @@
             else:
                 z_nat[p, pl.ds(b, 7, stride=NB), :] = z0[b, :7]
         return carry
-    lax.fori_loop(0, N, start_own, 0)
+    planes(0, N, start_own, 0)
 
     def start_ghost(p, carry):
         diag_of(p)
@@ -404,7 +419,7 @@
 
     z_y = send(7, z_nat.at[pl.ds(0, N), pl.ds(near_y, SUB), :], z_nat.at[pl.ds(0, N), pl.ds(N, SUB), :], (0, 1, 0))
     pack(z_nat, zs.at[1], ds_.at[1])
-    lax.fori_loop(N, E, start_ghost, 0)
+    planes(N, E, start_ghost, 0)
     z_z = send(SUB, zs.at[1], zr.at[1], (0, 0, 1))
     z_d = send(TILES, ds_.at[1], dr.at[1], (0, 1, 1))
     z_y.wait()
@@ -421,7 +436,7 @@
         z_p = jnp.where(jnp.logical_and(p == 0, cx == 0), 0.0, load_chunk(z_nat, before))
         z_n = jnp.where(jnp.logical_and(p == N - 1, cx == 1), 0.0, load_chunk(z_nat, after))
         b0 = inv * divergence(h_x, h_xn, h_y, h_z, load_chunk(z_nat, p), z_p, z_n, None, None)
-        b_a[0, p] = b0
+        b_a[0][p + 1] = b0
         cut = jnp.logical_or(jnp.logical_and(p == 0, cx == 0), jnp.logical_and(p == N, cx == 1))
         twice = 2.0 * inv
         cx_a[p] = jnp.where(cut, 0.0, h_x * (twice * isd_a[before]))
@@ -438,33 +453,38 @@
         return tuple(c + n for c, n in zip(carry, new))
 
     zero = jnp.zeros((SUB, LANES), F32)
-    sums = lax.fori_loop(0, N, functools.partial(first, True), (zero,) * 6)
-    lax.fori_loop(N, E, functools.partial(first, False), 0)
+
+    def wrap(ref):
+        ref[0] = ref[E]
+        ref[E + 1] = ref[1]
+    sums = planes(0, N, functools.partial(first, True), (zero,) * 6)
+    planes(N, E, functools.partial(first, False), 0)
     cx_a[E] = cx_a[0]
+    wrap(b_a[0])
     acc[0] = own_cells(sums[0], sums[1])
     acc[1] = own_cells(sums[2], sums[3])
     acc[TILES] = own_cells(sums[4], sums[5])
     acc[23] = zero
 
     def advance(k, own, p, carry):
-        before = jnp.where(p == 0, E - 1, p - 1)
-        after = jnp.where(p == E - 1, 0, p + 1)
-        v = b_a[k - 1, p]
+        old, here = b_a[k - 1], p + 1
+        v = old[here]
         c_y, c_z = cy_a[p], cz_a[p]
-        new = cx_a[p] * b_a[k - 1, before] + cx_a[p + 1] * b_a[k - 1, after]
+        new = cx_a[p] * old[here - 1] + cx_a[p + 1] * old[here + 1]
         new = new + (c_y * row_down(v) + row_up(c_y * v))
         new = new + (c_z * lane_down(v) + lane_up(c_z * v))
-        new = 0.5 * new if k == 1 else new - b_a[k - 2, p]
-        b_a[k, p] = new
+        new = 0.5 * new if k == 1 else new - b_a[k - 2][here]
+        b_a[k][here] = new
         if not own:
             return carry
         dots = dot_pair(v0_a[p], new) + dot_pair(v, new) + dot_pair(new, new)
         return tuple(c + n for c, n in zip(carry, dots))
 
     for k in range(1, STEPS):
-        sums = lax.fori_loop(0, N, functools.partial(advance, k, True), (zero,) * 6)
+        sums = planes(0, N, functools.partial(advance, k, True), (zero,) * 6)
         if k < STEPS - 1:
-            lax.fori_loop(N, E, functools.partial(advance, k, False), 0)
+            planes(N, E, functools.partial(advance, k, False), 0)
+            wrap(b_a[k])
         acc[1 + k] = own_cells(sums[0], sums[1])
         acc[16 + k - 1] = own_cells(sums[2], sums[3])
         if k < STEPS - 1:
@@ -537,8 +557,9 @@
         carry = list(carry)
         for b0 in range(0, NB, 2):
             cut = pl.ds(b0, 2)
-            v0, sd = v0_a[p, cut], sd_a[p, cut]
-            bs = [b_a[j, p, cut] for j in range(SUB)]
+            v0 = v0_a[p, cut]
+            sd = jnp.stack([k_nat[p, pl.ds(SUB * (b0 + b), SUB), :] for b in range(2)], axis=0)
+            bs = [ref[p + 1, cut] for ref in b_a]
             for t in range(STEPS):
                 y = v0
                 for j in range(t + 1):
@@ -574,7 +595,7 @@
             cut = pl.ds(b0, 2)
             x = coef[slot['x', 0]] * v0_a[p, cut]
             for j in range(1, SUB):
-                x = x + coef[slot['x', j]] * b_a[j - 1, p, cut]
+                x = x + coef[slot['x', j]] * b_a[j - 1][p + 1, cut]
             x = x * isd_a[p, cut]
             u = jnp.stack([u_nat[p, pl.ds(b0 + b, SUB, stride=NB), :] for b in range(2)], axis=0)
             put(k_in, p, b0, u + x)
@@ -589,7 +610,7 @@
     for dev in range(1, SUB):
         part = part + rgath[dev]
     part = jnp.broadcast_to(jnp.sum(part, axis=1, keepdims=True), (SUB, LANES))
-    rr_ref[...] = part
+    rr_ref[...] = jnp.sum(jnp.where(lane == sub, part, 0.0), axis=0, keepdims=True)[:, :STEPS]
     for copy in outs:
         copy.wait()
 
@@ -598,7 +619,6 @@
     spec = P('gx', 'gy', 'gz')
 
     def local(k_cell, k_ghost, f_rhs, u_init):
-        kgt = jnp.swapaxes(k_ghost[4:6], 1, 2)
         big = (E, NB, SUB, LANES)
         ext = (E + 1, NB, SUB, LANES)
         vm = lambda *shape: pltpu.VMEM(shape, F32)
@@ -606,13 +626,14 @@
         block = jax.ShapeDtypeStruct((N, N, N), F32)
         u, r, rr = pl.pallas_call(
             kernel,
-            out_shape=(block, block, jax.ShapeDtypeStruct((SUB, LANES), F32)),
-            in_specs=[any_spec] * 5,
+            out_shape=(block, block, jax.ShapeDtypeStruct((1, STEPS), F32)),
+            in_specs=[any_spec] * 4,
             out_specs=(any_spec, any_spec, pl.BlockSpec(memory_space=pltpu.VMEM)),
             scratch_shapes=[
                 vm(N, N, N), vm(N, N, N), vm(N, N, N), vm(E + 1, E, LANES), vm(E, E, LANES), vm(E, E, LANES),
-                vm(*ext), vm(*big), vm(*big), vm(*big), vm(N, NB, SUB, LANES), vm(N, NB, SUB, LANES), vm(SUB, *big),
-                vm(3, 144, 144), vm(E, LANES), vm(E, LANES), vm(N, SUB, N), vm(1, N, N),
+                vm(*ext), vm(*big), vm(*big), vm(*big), vm(N, NB, SUB, LANES),
+                *[vm(E + 2, NB, SUB, LANES)] * STEPS,
+                vm(3, 144, 144), vm(LANES, LANES), vm(LANES, LANES), vm(E, LANES), vm(N, SUB, N), vm(1, N, N),
                 vm(2, 45, SUB, LANES), vm(2, 45, SUB, LANES), vm(2, TILES, SUB, LANES), vm(2, TILES, SUB, LANES),
                 vm(N, N), vm(N, N), vm(TILES, SUB, LANES), vm(TILES, SUB, LANES),
                 vm(NDOT, SUB, LANES), vm(SUB, 2 * NDOT, LANES), vm(SUB, SUB, LANES), vm(SUB, SUB, LANES), vm(44, SUB, LANES),
@@ -621,7 +642,7 @@
                 pltpu.SemaphoreType.DMA((2, 7)), pltpu.SemaphoreType.DMA((2, 7)),
             ],
             compiler_params=pltpu.CompilerParams(collective_id=0, has_side_effects=True, vmem_limit_bytes=67043328),
-        )(k_cell, f_rhs, u_init, k_ghost, kgt)
-        return u, r, rr[:, 0]
+        )(k_cell, f_rhs, u_init, k_ghost)
+        return u, r, rr.reshape(STEPS)
 
     return jax.shard_map(local, mesh=mesh, in_specs=(spec, P(), spec, spec), out_specs=(spec, spec, P()), check_vma=False)

time: 146 us -> 95.3 us (0.65)
  Pallas kernels: 137 us -> 89 us
  local copies, waits for them, and re-layouts: 8.24 us -> 5.59 us
    pallas_call x1, Pallas kernels: 137 us -> 89 us  [local(): pl.pallas_call(kernel, out_shape=(block, block, jax.ShapeDtypeStruct((1,...]
    slice x2 -> x0, local copies, waits for them, and re-layouts: 2.28 us -> none  [the longest x1 1.3 us: local(): return (u, r, rr[:, 0])]
    unnamed x5 -> x7, local copies, waits for them, and re-layouts: 5.96 us -> 5.59 us
where the time goes in v2:
time: 95.3 us; the launch traced here: 95.2 us
  Pallas kernels  89 us (93%)
  local copies, waits for them, and re-layouts  5.59 us (6%)
    pallas_call x1, Pallas kernels, local(): pl.pallas_call(kernel, out_shape=(block, block, jax.ShapeDtypeStruct((1,...  89 us
    unnamed x7, local copies, waits for them, and re-layouts  5.59 us

profile of v2, /device:TPU:0, one launch (start us, length us, event | category | flops | bytes accessed | tf_op | source)
XLA Modules:
  0.0 95.2 jit_solution(18390415564740961056)
XLA Ops:
  0.6 89.0 %shard_map.67 = (f32[72,72,72]{2,1,0:T(8,128)}, f32[72,72,72]{2,1,0:T(8,128)}, f32[1,8]{1,0:T(1,128)}) custom-call(f32[72,72,72]{2,1,0:T(8,128)} %k_hbm.1, f32[72,72,72]{2,1,0:T(8,128)} %f_hbm.1, f32[72,72,72]{2,1,0:T(8,128)} %u_hbm.1, f32[6,144,144]{2,1,0:T(8,128)} %kg_hbm.1), custom_call_target="tpu_custom_call" | custom-call | tf_op jit(solution)/shard_map/pallas_call | solution.py:627
  89.6 0.0 copy-start
  89.6 3.6 %copy.10 = f32[72,72,72]{2,1,0:T(8,128)} copy(f32[72,72,72]{2,1,0:T(8,128)} %get-tuple-element.12) | data formatting | bytes 2985984
  93.2 0.0 copy-done
  93.2 0.0 copy-start.1
  93.2 1.5 %copy.11 = f32[72,72,72]{2,1,0:T(8,128)} copy(f32[72,72,72]{2,1,0:T(8,128)S(1)} %copy-done) | data formatting | bytes 2985984
  94.7 0.0 copy-done.1
  94.7 0.5 copy.12
Async XLA Ops:
  89.6 3.6 %copy-start = (f32[72,72,72]{2,1,0:T(8,128)S(1)}, f32[72,72,72]{2,1,0:T(8,128)}, u32[]{:S(2)}) copy-start(f32[72,72,72]{2,1,0:T(8,128)} %get-tuple-element.13) | copy-start | bytes 4478980
  93.2 1.5 %copy-start.1 = (f32[1,8]{1,0:T(1,128)S(1)}, f32[1,8]{1,0:T(1,128)}, u32[]{:S(2)}) copy-start(f32[1,8]{1,0:T(1,128)} %get-tuple-element.8) | copy-start | bytes 100

commit v3 on v2

v3 whole, which is shorter than its diff:
```python
import functools

import jax
import jax.numpy as jnp
from jax import lax
from jax.experimental import pallas as pl
from jax.experimental.pallas import tpu as pltpu
from jax.sharding import PartitionSpec as P


N = 72
H = 8
E = N + H
NB = 10
STEPS = 8
MESH = pl.DeviceIdType.MESH
F32 = jnp.float32
OTHERS = [(fx, fy, fz) for fx in (0, 1) for fy in (0, 1) for fz in (0, 1) if fx or fy or fz]
NDOT = 24
SUB = 8
LANES = 128
TILES = 9
PART = 24
WIDTH = 4
LAST = 7
GROUPS = 16
PIECES = 5
ZERO, ONE, HALF, TWO = 0.0, 1.0, 0.5, 2.0


def iota(axis):
    return lax.broadcasted_iota(jnp.int32, (SUB, LANES), axis)


def two_sum(a, b):
    s = a + b
    t = s - a
    return s, (a - (s - t)) + (b - t)


def quick(a, b):
    s = a + b
    return s, b - (s - a)


def two_prod(a, b):
    def split(x):
        t = x * 4097.0
        hi = t - (t - x)
        return hi, x - hi
    p = a * b
    ah, al = split(a)
    bh, bl = split(b)
    return p, ((ah * bh - p) + ah * bl + al * bh) + al * bl


def dadd(x, y):
    (xh, xl), (yh, yl) = x, y
    s, e = two_sum(xh, yh)
    return quick(s, e + (xl + yl))


def dsub(x, y):
    yh, yl = y
    return dadd(x, (-yh, -yl))


def dscale(x, c):
    hi, lo = x
    return hi * c, lo * c


def dmul(x, y):
    (xh, xl), (yh, yl) = x, y
    p, e = two_prod(xh, yh)
    return quick(p, e + (xh * yl + xl * yh))


def ddiv(x, y):
    (xh, xl), (yh, yl) = x, y
    q = xh / yh
    p, e = two_prod(q, yh)
    rest = ((xh - p) - e) + (xl - q * yl)
    return quick(q, rest / yh)


def step_lengths(m):
    alphas, betas = [], []
    y = dict(enumerate(m))
    p = {0: dsub(y[0], y[1])}
    for l in range(1, 15):
        p[l] = dsub(y[l], dscale(dadd(y[l + 1], y[l - 1]), HALF))
    for t in range(STEPS):
        alpha = ddiv(y[t], p[t])
        alphas.append(alpha[0])
        if t == STEPS - 1:
            break
        y_next = {l: dsub(y[l], dmul(alpha, p[l])) for l in range(t + 1, 15 - t)}
        beta = ddiv(y_next[t + 1], p[t])
        if t:
            beta = dscale(beta, HALF)
        betas.append(beta[0])
        p_next = {}
        for l in range(t + 1, 14 - t):
            side = y_next[l + 1] if l == t + 1 else dadd(y_next[l + 1], y_next[l - 1])
            p_next[l] = dadd(dsub(y_next[l], dscale(side, HALF)), dmul(beta, p[l]))
        y, p = y_next, p_next
    return alphas, betas


def basis_coefs(alphas, betas):
    def add(a, b):
        return b if a is None else (a if b is None else a + b)

    def axpy(x, c, y):
        return [xi if yi is None else (c * yi if xi is None else xi + c * yi) for xi, yi in zip(x, y)]

    def apply_op(v):
        out = [None] * 11
        out[1] = v[0]
        for j in range(SUB):
            if v[1 + j] is None:
                continue
            c = v[1 + j]
            out[1 + j] = add(out[1 + j], c)
            if j == 0:
                out[2] = add(out[2], -c)
            else:
                half = -HALF * c
                out[2 + j] = add(out[2 + j], half)
                out[j] = add(out[j], half)
        return out[:TILES]

    one = jnp.ones_like(alphas[0])
    y = [one] + [None] * SUB
    p = list(y)
    x = [None] * TILES
    ys = []
    for t in range(STEPS):
        q = apply_op(p)
        x = axpy(x, alphas[t], p)
        y = axpy(y, -alphas[t], q)
        ys.append(y)
        if t < STEPS - 1:
            p = axpy(y, betas[t], p)
    return ys, x


def row_down(v):
    return jnp.concatenate([pltpu.roll(v[NB - 1], 1, 0)[None], v[:NB - 1]], axis=0)


def row_up(v):
    return jnp.concatenate([v[1:], pltpu.roll(v[0], LAST, 0)[None]], axis=0)


def lane_down(v):
    return pltpu.roll(v, 1, 2)


def lane_up(v):
    return pltpu.roll(v, 127, 2)


def load_chunk(ref, plane):
    return jnp.stack([ref[plane, pl.ds(b, SUB, stride=NB), :] for b in range(NB)], axis=0)


def replace(v, b, mask, value):
    return jnp.concatenate(([v[:b]] if b else []) + [jnp.where(mask, value, v[b])[None], v[b + 1:]], axis=0)


def harmonic(a, b):
    return TWO * a * b / (a + b)


def dot_pair(a, b):
    prod = a * b
    return jnp.sum(prod[:2], axis=0), jnp.sum(prod[2:], axis=0)


def pick(mask, a, b):
    return lax.select_n(mask, b, a)


def planes(lo, hi, body, init, width=WIDTH):
    def some(n, carry):
        for w in range(width):
            carry = body(lo + n * width + w, carry)
        return carry
    return lax.fori_loop(0, (hi - lo) // width, some, init)


def own_cells(low, high):
    sub, lane = iota(0), iota(1)
    return jnp.where(lane < N, low + jnp.where(sub < LAST, high, ZERO), ZERO)


def kernel(k_hbm, f_hbm, u_hbm, kg_hbm, uo_hbm, ro_hbm, rr_ref,
           k_in, u_in, f_in, k_nat, u_nat, z_nat, cx_a, cy_a, cz_a, isd_a, v0_a, b0_a, b1_a, b2_a, b3_a, b4_a, b5_a, b6_a, b7_a,
           walls, wz, wz_t, wy, ky, kx, ux, zs, zr, ds_, dr, row_s, row_r, lane_s, lane_r, acc, gath, rsend, rgath, coef,
           load_sem, out_sem, send_sem, recv_sem, all_send, all_recv):
    cx, cy, cz = lax.axis_index('gx'), lax.axis_index('gy'), lax.axis_index('gz')
    me = cx + 2 * cy + 4 * cz
    b_a = (b0_a, b1_a, b2_a, b3_a, b4_a, b5_a, b6_a, b7_a)
    lane, sub = iota(1), iota(0)

    def peer(fx, fy, fz):
        out = {}
        if fx:
            out['gx'] = 1 - cx
        if fy:
            out['gy'] = 1 - cy
        if fz:
            out['gz'] = 1 - cz
        return out

    loads = []
    for n, (src, dst) in enumerate([(k_hbm, k_in), (u_hbm, u_in), (f_hbm, f_in)]):
        loads.append(pltpu.make_async_copy(src, dst, load_sem.at[n]))
    loads.append(pltpu.make_async_copy(kg_hbm.at[cx], walls.at[0], load_sem.at[3]))
    loads.append(pltpu.make_async_copy(kg_hbm.at[2 + cy], walls.at[1], load_sem.at[4]))
    loads.append(pltpu.make_async_copy(kg_hbm.at[4 + cz], walls.at[2], load_sem.at[PIECES]))
    for n in (0, 1, 3, 4, PIECES, 2):
        loads[n].start()

    barrier = pltpu.get_barrier_semaphore()
    for flips in OTHERS:
        pl.semaphore_signal(barrier, inc=1, device_id=peer(*flips), device_id_type=MESH)
    pl.semaphore_wait(barrier, len(OTHERS))

    def send(n, src, dst, flips):
        copy = pltpu.make_async_remote_copy(src_ref=src, dst_ref=dst, send_sem=send_sem.at[n], recv_sem=recv_sem.at[n],
                                            device_id=peer(*flips), device_id_type=MESH)
        copy.start()
        return copy

    near_y = pl.multiple_of((N - H) * (1 - cy), SUB)
    near_x = (N - H) * (1 - cx)
    group8 = lane // SUB
    src8 = (N - H) * (1 - cz)
    dst8 = N + 48 * cz
    ghost8 = jnp.logical_and(lane >= dst8, lane < dst8 + SUB)
    wall_lane = 127 - 55 * cz
    own_lane = lane < N
    at_wall = lane == wall_lane
    zero = jnp.zeros((SUB, LANES), F32)
    ones = jnp.ones((SUB, LANES), F32)

    def turn(x, by):
        return pltpu.roll(x, lax.rem(by + LANES, LANES), 1)

    def widen(x):
        return x if x.shape[1] == LANES else jnp.concatenate([x, jnp.zeros((x.shape[0], LANES - x.shape[1]), F32)], axis=1)

    def pack(nat, packed, corner):
        groups = [group8 == g for g in range(GROUPS)]

        def body(o, carry):
            for q in range(PIECES):
                out = None
                for g in range(min(GROUPS, N - GROUPS * q)):
                    t = GROUPS * q + g
                    if t % TILES == 0:
                        plane = widen(nat[o * SUB + t // TILES, 0:N, :])
                    x = turn(plane[SUB * (t % TILES):SUB * (t % TILES) + SUB], SUB * g - src8)
                    out = x if g == 0 else pick(groups[g], x, out)
                packed[o * PIECES + q] = out
            out = None
            for g in range(SUB):
                x = widen(nat[o * SUB + g, pl.ds(near_y, SUB), :])
                x = turn(x, SUB * g - src8)
                out = x if g == 0 else pick(groups[g], x, out)
            corner[o] = out
            return carry
        lax.fori_loop(0, TILES, body, 0)

    def unpack(own, side, nat, packed, corner, fill, wall, o, carry):
        packs, corner_in = [packed[o * PIECES + q] for q in range(PIECES)], corner[o]
        for pi in range(SUB):
            i, out = o * SUB + pi, []
            plane = widen(own[i, 0:N, :])
            for jt in range(NB):
                if jt < TILES:
                    t = pi * TILES + jt
                    got, g = packs[t // GROUPS], t % GROUPS
                else:
                    got, g = corner_in, pi
                x = plane[SUB * jt:SUB * jt + SUB] if jt < TILES else widen(side[i])
                other = fill if wall is None else pick(at_wall, wall_column(i, jt), fill)
                out.append(pick(own_lane, x, pick(ghost8, turn(got, dst8 - SUB * g), other)))
            nat[i, 0:E, :] = jnp.concatenate(out, axis=0)
        return carry

    def wall_column(i, jt):
        at = SUB * jt if jt < TILES else pl.multiple_of(N + 48 * cy, SUB)
        return turn(wz_t[pl.ds(at, SUB), :], wall_lane - i)

    loads[0].wait()
    loads[1].wait()
    last_x, last_y, last_z = (N - 1) * (1 - cx), (N - 1) * (1 - cy), (N - 1) * (1 - cz)
    one_x = [send(0, k_in.at[pl.ds(last_x, 1)], kx, (1, 0, 0)), send(1, u_in.at[pl.ds(last_x, 1)], ux, (1, 0, 0))]

    def pack_one(o, carry):
        for n, src in enumerate((k_in, u_in)):
            row_s[n, pl.ds(pl.multiple_of(o * SUB, SUB), SUB), :] = jnp.concatenate(
                [src[o * SUB + r, pl.ds(last_y, 1), :] for r in range(SUB)], axis=0)
            out = None
            for t in range(N):
                if t % TILES == 0:
                    plane = widen(src[o * SUB + t // TILES])
                x = turn(plane[SUB * (t % TILES):SUB * (t % TILES) + SUB], t - last_z)
                out = x if t == 0 else pick(lane == t, x, out)
            lane_s[n, o] = out
        return carry
    lax.fori_loop(0, TILES, pack_one, 0)
    one_y = send(2, row_s, row_r, (0, 1, 0))
    one_z = send(3, lane_s, lane_r, (0, 0, 1))
    k_y = send(4, k_in.at[:, pl.ds(near_y, SUB), :], ky, (0, 1, 0))
    pack(k_in, zs.at[0], ds_.at[0])
    k_z = send(PIECES, zs.at[0], zr.at[0], (0, 0, 1))
    k_d = send(6, ds_.at[0], dr.at[0], (0, 1, 1))

    for n in (3, 4, PIECES):
        loads[n].wait()

    def lane_ring(w, at, c):
        left, right = walls[w, pl.ds(at, SUB), 0:LANES], walls[w, pl.ds(at, SUB), LANES:144]
        gap = jnp.zeros((SUB, 56), F32)
        right = jnp.concatenate([gap, right, gap], axis=1)
        turned = jnp.where(jnp.logical_and(lane >= 56, lane < N), right, pltpu.roll(left, 56, 1))
        return jnp.where(c == 0, left, turned)

    for jt in range(NB):
        at_j = pl.multiple_of(N * cy + SUB * jt if jt < TILES else N - H * cy, SUB)
        at_i = pl.multiple_of(N * cx + SUB * jt if jt < TILES else N - H * cx, SUB)
        k_nat[E, pl.ds(SUB * jt, SUB), :] = lane_ring(0, at_j, cz)
        wy[pl.ds(SUB * jt, SUB), :] = lane_ring(1, at_i, cz)
        if jt < TILES:
            wz[pl.ds(SUB * jt, SUB), :] = lane_ring(2, at_i, cy)
    wz_t[...] = wz[...].T

    loads[2].wait()

    def take_f(p, carry):
        for b in range(NB):
            rows = SUB if b < 2 else LAST
            v0_a[p, b, 0:rows, 0:N] = f_in[p, pl.ds(b, rows, stride=NB), :]
        return carry
    planes(0, N, take_f, 0)

    u_nat[E - 1 - LAST * cx] = jnp.zeros((E, LANES), F32)
    one_lane = N + 55 * cz
    at_one = lane == one_lane
    for copy in one_x + [one_y, one_z]:
        copy.wait()
    u_nat[N + LAST * cx, 0:N, 0:N] = ux[0]
    k_nat[E + 1, 0:N, 0:N] = kx[0]

    def unpack_one(o, carry):
        lanes_in = [lane_r[n, o] for n in range(2)]
        for pi in range(SUB):
            i = o * SUB + pi
            planes_in = [widen(k_in[i]), widen(u_in[i])]
            for n, nat in enumerate((k_nat, u_nat)):
                out = []
                for jt in range(TILES):
                    other = zero if n else pick(at_wall, wall_column(i, jt), ones)
                    other = pick(at_one, turn(lanes_in[n], one_lane - (pi * TILES + jt)), other)
                    out.append(pick(own_lane, planes_in[n][SUB * jt:SUB * jt + SUB], other))
                nat[i, 0:N, :] = jnp.concatenate(out, axis=0)
        return carry
    lax.fori_loop(0, TILES, unpack_one, 0)

    row0 = sub == 0
    row72 = sub == LAST

    def divergence(h_x, h_xn, h_y, h_z, v, v_prev, v_next, low_row, high_row):
        low = row_down(v)
        high = v
        if low_row is not None:
            low = replace(low, 0, row0, low_row)
            high = replace(v, 2, row72, high_row)
        else:
            low = replace(low, 0, jnp.logical_and(row0, cy == 0), ZERO)
            high = replace(v, 2, jnp.logical_and(row72, cy == 1), ZERO)
        f_y = h_y * (high - low)
        f_z = h_z * (v - lane_down(v))
        return ((h_x * (v - v_prev) - h_xn * (v_next - v)) + (f_y - row_up(f_y))) + (f_z - lane_up(f_z))

    def full(row):
        return jnp.broadcast_to(widen(row), (SUB, LANES))

    def add_up(h_x, h_xn, h_y, h_z):
        return ((h_x + h_xn) + (h_y + row_up(h_y))) + (h_z + lane_up(h_z))

    def start_own(n, carry):
        p0 = WIDTH * n
        first_trip, last_trip = n == 0, n == N // WIDTH - 1
        k_p = [load_chunk(k_nat, jnp.where(first_trip, E + cx, p0 - 1))]
        u_p = [load_chunk(u_nat, jnp.where(first_trip, E - 1, p0 - 1))]
        for w in range(WIDTH):
            k_p.append(load_chunk(k_nat, p0 + w))
            u_p.append(load_chunk(u_nat, p0 + w))
        k_p.append(load_chunk(k_nat, jnp.where(last_trip, E + 1 - cx, p0 + WIDTH)))
        u_p.append(load_chunk(u_nat, p0 + WIDTH))
        h_x = [harmonic(k_p[w + 1], k_p[w]) for w in range(WIDTH + 1)]
        for w in range(WIDTH):
            p, kc = p0 + w, k_p[w + 1]
            wall, got = full(wy[pl.ds(p, 1), :]), full(row_r[0, pl.ds(p, 1), :])
            low = replace(row_down(kc), 0, row0, jnp.where(cy == 0, wall, got))
            high = replace(kc, 2, row72, jnp.where(cy == 0, got, wall))
            h_y = harmonic(high, low)
            h_z = harmonic(kc, lane_down(kc))
            inv = lax.rsqrt(add_up(h_x[w], h_x[w + 1], h_y, h_z))
            got = full(row_r[1, pl.ds(p, 1), :])
            a_u = divergence(h_x[w], h_x[w + 1], h_y, h_z, u_p[w + 1], u_p[w], u_p[w + 2],
                             jnp.where(cy == 0, ZERO, got), jnp.where(cy == 0, got, ZERO))
            y0 = (v0_a[p] - a_u) * inv
            v0_a[p] = y0
            z0 = y0 * inv
            for b in range(NB):
                if b < 2:
                    z_nat[p, pl.ds(b, SUB, stride=NB), :] = z0[b]
                else:
                    z_nat[p, pl.ds(b, LAST, stride=NB), :] = z0[b, :LAST]
        return carry
    lax.fori_loop(0, N // WIDTH, start_own, 0)

    z_y = send(LAST, z_nat.at[pl.ds(0, N), pl.ds(near_y, SUB), :], z_nat.at[pl.ds(0, N), pl.ds(N, SUB), :], (0, 1, 0))
    pack(z_nat, zs.at[1], ds_.at[1])
    z_z = send(8, zs.at[1], zr.at[1], (0, 0, 1))
    z_d = send(9, ds_.at[1], dr.at[1], (0, 1, 1))

    def spread(n, nat, take):
        take(SUB * (1 - cx), 0)
        copy = send(n, nat.at[pl.ds(near_x, SUB)], nat.at[pl.ds(N, SUB)], (1, 0, 0))
        lax.fori_loop(0, SUB, lambda o, carry: take(o + cx, carry), 0)
        return copy

    for copy in (k_y, k_z, k_d):
        copy.wait()
    spread(NB, k_nat, functools.partial(unpack, k_in, ky, k_nat, zr.at[0], dr.at[0], ones, wz_t)).wait()

    def faces(p, carry):
        kc = load_chunk(k_nat, p)
        before = jnp.where(jnp.logical_and(p == 0, cx == 0), E, jnp.where(p == 0, E - 1, p - 1))
        here = jnp.where(jnp.logical_and(p == N, cx == 1), E, p)
        cx_a[p] = harmonic(load_chunk(k_nat, here), load_chunk(k_nat, before))
        wall = full(wy[pl.ds(p, 1), :])
        low = replace(row_down(kc), 0, jnp.logical_and(row0, cy == 0), wall)
        high = replace(kc, 2, jnp.logical_and(row72, cy == 1), wall)
        cy_a[p] = harmonic(high, low)
        cz_a[p] = harmonic(kc, lane_down(kc))
        return carry
    planes(0, E, faces, 0)
    cx_a[E] = cx_a[0]
    cx_a[E + 1] = cx_a[1]

    def scales(own, p, carry):
        d = add_up(cx_a[p], cx_a[p + 1], cy_a[p], cz_a[p])
        inv = lax.rsqrt(d)
        isd_a[p] = inv
        if own:
            sd = d * inv
            for b in range(NB):
                k_nat[p, pl.ds(SUB * b, SUB), :] = sd[b]
        return carry
    planes(0, N, functools.partial(scales, True), 0)
    planes(N, E, functools.partial(scales, False), 0)

    for copy in (z_y, z_z, z_d):
        copy.wait()
    z_x = spread(11, z_nat, functools.partial(unpack, z_nat, z_nat.at[:, pl.ds(N, SUB), :], z_nat, zr.at[1], dr.at[1],
                                              zero, None))

    def first(own, p, carry):
        static = isinstance(p, int)
        before = (p - 1) % E if static else p - 1
        after = p + 1 if static else lax.rem(p + 1, E)
        h_x, h_xn, h_y, h_z, inv = cx_a[p], cx_a[E + 1 if static and p == 0 else p + 1], cy_a[p], cz_a[p], isd_a[p]
        z_p = jnp.where(jnp.logical_and(p == 0, cx == 0), ZERO, load_chunk(z_nat, before))
        z_n = jnp.where(jnp.logical_and(p == N - 1, cx == 1), ZERO, load_chunk(z_nat, after))
        b0 = inv * divergence(h_x, h_xn, h_y, h_z, load_chunk(z_nat, p), z_p, z_n, None, None)
        b_a[0][p + 1] = b0
        cut = jnp.logical_or(jnp.logical_and(p == 0, cx == 0), jnp.logical_and(p == N, cx == 1))
        twice = TWO * inv
        cx_a[p] = jnp.where(cut, ZERO, h_x * (twice * isd_a[before]))
        c_y = h_y * (twice * row_down(inv))
        c_y = replace(c_y, 0, jnp.logical_and(row0, cy == 0), ZERO)
        cy_a[p] = replace(c_y, 2, jnp.logical_and(row72, cy == 1), ZERO)
        c_z = h_z * (twice * lane_down(inv))
        edge = N * cz
        cz_a[p] = jnp.where(lax.broadcasted_iota(jnp.int32, (NB, SUB, LANES), 2) == edge, ZERO, c_z)
        if not own:
            return carry
        v0 = v0_a[p]
        new = dot_pair(v0, v0) + dot_pair(v0, b0) + dot_pair(b0, b0)
        return tuple(c + n for c, n in zip(carry, new))


    def wrap(ref):
        ref[0] = ref[E]
        ref[E + 1] = ref[1]
    sums = planes(1, N - 1, functools.partial(first, True), (zero,) * 6, PIECES)
    z_x.wait()
    for p in (0, N - 1):
        sums = first(True, p, sums)
    planes(N, E, functools.partial(first, False), 0)
    cx_a[E] = cx_a[0]
    wrap(b_a[0])
    acc[0] = own_cells(sums[0], sums[1])
    acc[1] = own_cells(sums[2], sums[3])
    acc[TILES] = own_cells(sums[4], sums[PIECES])
    acc[23] = zero

    def advance(k, own, p, carry):
        old, here = b_a[k - 1], p + 1
        v = old[here]
        c_y, c_z = cy_a[p], cz_a[p]
        new = cx_a[p] * old[here - 1] + cx_a[p + 1] * old[here + 1]
        new = new + (c_y * row_down(v) + row_up(c_y * v))
        new = new + (c_z * lane_down(v) + lane_up(c_z * v))
        new = HALF * new if k == 1 else new - b_a[k - 2][here]
        b_a[k][here] = new
        if not own:
            return carry
        dots = dot_pair(v0_a[p], new) + dot_pair(v, new) + dot_pair(new, new)
        return tuple(c + n for c, n in zip(carry, dots))

    for k in range(1, STEPS):
        sums = planes(0, N, functools.partial(advance, k, True), (zero,) * 6)
        if k < STEPS - 1:
            planes(N, E, functools.partial(advance, k, False), 0)
            wrap(b_a[k])
        acc[1 + k] = own_cells(sums[0], sums[1])
        acc[GROUPS + k - 1] = own_cells(sums[2], sums[3])
        if k < STEPS - 1:
            acc[TILES + k] = own_cells(sums[4], sums[PIECES])

    def gather(buf, n_sem):
        copies = []
        for n, flips in enumerate(OTHERS):
            copies.append(pltpu.make_async_remote_copy(
                src_ref=buf.at[me], dst_ref=buf.at[me], send_sem=all_send.at[n_sem, n], recv_sem=all_recv.at[n_sem, n],
                device_id=peer(*flips), device_id_type=MESH))
        for copy in copies:
            copy.start()
        return copies

    hi = acc[:, 0, :]
    lo = jnp.zeros((NDOT, LANES), F32)
    for s in range(1, SUB):
        hi, err = two_sum(hi, acc[:, s, :])
        lo = lo + err
    gath[me, 0:NDOT] = hi
    gath[me, NDOT:2 * NDOT] = lo
    for copy in gather(gath, 0):
        copy.wait()
    hi, lo = gath[0, 0:NDOT], gath[0, NDOT:2 * NDOT]
    for dev in range(1, SUB):
        hi, err = two_sum(hi, gath[dev, 0:NDOT])
        lo = lo + (gath[dev, NDOT:2 * NDOT] + err)
    for shift in (64, 32, GROUPS, SUB, 4, 2, 1):
        hi, err = two_sum(hi, pltpu.roll(hi, shift, 1))
        lo = (lo + pltpu.roll(lo, shift, 1)) + err
    hi, lo = quick(hi, lo)
    size = hi[0:1]
    factor = jnp.where(size > 1e30, TWO ** -110, jnp.where(size > 1e12, TWO ** -60, jnp.where(
        size < 1e-30, TWO ** 110, jnp.where(size < 1e-12, TWO ** 60, ONE)))).astype(F32)
    hi, lo = hi * factor, lo * factor

    def total(row):
        return jnp.broadcast_to(hi[row:row + 1], (SUB, LANES)), jnp.broadcast_to(lo[row:row + 1], (SUB, LANES))

    n_mom = [total(TILES), total(GROUPS)]
    for j in range(1, LAST):
        n_mom.append(dsub(dscale(total(TILES + j), TWO), n_mom[0]))
        n_mom.append(dsub(dscale(total(GROUPS + j), TWO), n_mom[1]))
    l_mom = [total(1 + j) for j in range(SUB)]
    for j in range(LAST, 14):
        l_mom.append(dsub(dscale(dsub(l_mom[j], n_mom[j]), TWO), l_mom[j - 1]))
    m_mom = [total(0)]
    m_mom.append(dsub(m_mom[0], l_mom[0]))
    for j in range(1, 15):
        m_mom.append(dsub(dscale(dsub(m_mom[j], l_mom[j]), TWO), m_mom[j - 1]))
    ys, xs = basis_coefs(*step_lengths(m_mom))
    slot = {}
    for t in range(STEPS):
        for j in range(t + 1):
            slot[t, j] = len(slot)
            coef[slot[t, j]] = ys[t][1 + j]
    for j in range(SUB):
        slot['x', j] = len(slot)
        coef[slot['x', j]] = xs[j]

    def put(ref, p, b0, val):
        for b in range(val.shape[0]):
            if b0 + b < 2:
                ref[p, pl.ds(b0 + b, SUB, stride=NB), :] = val[b, :, :N]
            else:
                ref[p, pl.ds(b0 + b, LAST, stride=NB), :] = val[b, :LAST, :N]

    def residuals(p, carry):
        carry = list(carry)
        for b0 in range(0, NB, 2):
            cut = pl.ds(b0, 2)
            v0 = v0_a[p, cut]
            sd = jnp.stack([k_nat[p, pl.ds(SUB * (b0 + b), SUB), :] for b in range(2)], axis=0)
            bs = [ref[p + 1, cut] for ref in b_a]
            for t in range(STEPS):
                y = v0
                for j in range(t + 1):
                    y = y + coef[slot[t, j]] * bs[j]
                r = sd * y
                which = 2 * t + (b0 > 0)
                carry[which] = carry[which] + jnp.sum(r * r, axis=0)
                if t == STEPS - 1:
                    put(f_in, p, b0, r)
        return tuple(carry)

    outs = []

    def flush(n, nat, hbm, o):
        outs.append(pltpu.make_async_copy(nat.at[pl.ds(PART * o, PART)], hbm.at[pl.ds(PART * o, PART)],
                                          out_sem.at[n, o]))
        outs[-1].start()

    sums = (zero,) * GROUPS
    for o in range(3):
        sums = lax.fori_loop(PART * o, PART * o + PART, residuals, sums)
        flush(0, f_in, ro_hbm, o)
    for t in range(STEPS):
        rsend[t] = own_cells(sums[2 * t], sums[2 * t + 1])
    part = rsend[:, 0, :]
    for s in range(1, SUB):
        part = part + rsend[:, s, :]
    rgath[me] = part
    rr_copies = gather(rgath, 1)

    def update(p, carry):
        for b0 in range(0, NB, 2):
            cut = pl.ds(b0, 2)
            x = coef[slot['x', 0]] * v0_a[p, cut]
            for j in range(1, SUB):
                x = x + coef[slot['x', j]] * b_a[j - 1][p + 1, cut]
            x = x * isd_a[p, cut]
            u = jnp.stack([u_nat[p, pl.ds(b0 + b, SUB, stride=NB), :] for b in range(2)], axis=0)
            put(k_in, p, b0, u + x)
        return carry

    for o in range(3):
        lax.fori_loop(PART * o, PART * o + PART, update, 0)
        flush(1, k_in, uo_hbm, o)
    for copy in rr_copies:
        copy.wait()
    part = rgath[0]
    for dev in range(1, SUB):
        part = part + rgath[dev]
    part = jnp.broadcast_to(jnp.sum(part, axis=1, keepdims=True), (SUB, LANES))
    rr_ref[...] = jnp.sum(jnp.where(lane == sub, part, ZERO), axis=0, keepdims=True)[:, :STEPS]
    for copy in outs:
        copy.wait()


def solution(mesh):
    spec = P('gx', 'gy', 'gz')

    def local(k_cell, k_ghost, f_rhs, u_init):
        big = (E, NB, SUB, LANES)
        ext = (E + 2, NB, SUB, LANES)
        vm = lambda *shape: pltpu.VMEM(shape, F32)
        any_spec = pl.BlockSpec(memory_space=pl.ANY)
        block = jax.ShapeDtypeStruct((N, N, N), F32)
        u, r, rr = pl.pallas_call(
            kernel,
            out_shape=(block, block, jax.ShapeDtypeStruct((1, STEPS), F32)),
            in_specs=[any_spec] * 4,
            out_specs=(any_spec, any_spec, pl.BlockSpec(memory_space=pltpu.VMEM)),
            scratch_shapes=[
                vm(N, N, N), vm(N, N, N), vm(N, N, N), vm(E + 2, E, LANES), vm(E, E, LANES), vm(E, E, LANES),
                vm(*ext), vm(*big), vm(*big), vm(*big), vm(N, NB, SUB, LANES),
                *[vm(E + 2, NB, SUB, LANES)] * STEPS,
                vm(3, 144, 144), vm(LANES, LANES), vm(LANES, LANES), vm(E, LANES), vm(N, SUB, N), vm(1, N, N), vm(1, N, N),
                vm(2, 45, SUB, LANES), vm(2, 45, SUB, LANES), vm(2, TILES, SUB, LANES), vm(2, TILES, SUB, LANES),
                vm(2, N, N), vm(2, N, N), vm(2, TILES, SUB, LANES), vm(2, TILES, SUB, LANES),
                vm(NDOT, SUB, LANES), vm(SUB, 2 * NDOT, LANES), vm(SUB, SUB, LANES), vm(SUB, SUB, LANES), vm(44, SUB, LANES),
                pltpu.SemaphoreType.DMA((6,)), pltpu.SemaphoreType.DMA((2, 3)),
                pltpu.SemaphoreType.DMA((12,)), pltpu.SemaphoreType.DMA((12,)),
                pltpu.SemaphoreType.DMA((2, LAST)), pltpu.SemaphoreType.DMA((2, LAST)),
            ],
            compiler_params=pltpu.CompilerParams(collective_id=0, has_side_effects=True, vmem_limit_bytes=67043328),
        )(k_cell, f_rhs, u_init, k_ghost)
        return u, r, rr.reshape(STEPS)

    return jax.shard_map(local, mesh=mesh, in_specs=(spec, P(), spec, spec), out_specs=(spec, spec, P()), check_vma=False)
```

time: 95.3 us -> 83.8 us (0.88)
  Pallas kernels: 89 us -> 77.4 us
    pallas_call x1, Pallas kernels: 89 us -> 77.4 us  [local(): pl.pallas_call(kernel, out_shape=(block, block, jax.ShapeDtypeStruct((1,...]
where the time goes in v3:
time: 83.8 us; the launch traced here: 83.7 us
  Pallas kernels  77.4 us (92%)
  local copies, waits for them, and re-layouts  5.59 us (7%)
    pallas_call x1, Pallas kernels, local(): pl.pallas_call(kernel, out_shape=(block, block, jax.ShapeDtypeStruct((1,...  77.4 us
    unnamed x7, local copies, waits for them, and re-layouts  5.59 us

profile of v3, /device:TPU:0, one launch (start us, length us, event | category | flops | bytes accessed | tf_op | source)
XLA Modules:
  0.0 83.7 jit_solution(17490693634179837237)
XLA Ops:
  0.6 77.4 %shard_map.67 = (f32[72,72,72]{2,1,0:T(8,128)}, f32[72,72,72]{2,1,0:T(8,128)}, f32[1,8]{1,0:T(1,128)}) custom-call(f32[72,72,72]{2,1,0:T(8,128)} %k_hbm.1, f32[72,72,72]{2,1,0:T(8,128)} %f_hbm.1, f32[72,72,72]{2,1,0:T(8,128)} %u_hbm.1, f32[6,144,144]{2,1,0:T(8,128)} %kg_hbm.1), custom_call_target="tpu_custom_call" | custom-call | tf_op jit(solution)/shard_map/pallas_call | solution.py:675
  78.1 0.0 copy-start
  78.1 3.6 %copy.10 = f32[72,72,72]{2,1,0:T(8,128)} copy(f32[72,72,72]{2,1,0:T(8,128)} %get-tuple-element.12) | data formatting | bytes 2985984
  81.6 0.0 copy-done
  81.7 0.0 copy-start.1
  81.7 1.5 %copy.11 = f32[72,72,72]{2,1,0:T(8,128)} copy(f32[72,72,72]{2,1,0:T(8,128)S(1)} %copy-done) | data formatting | bytes 2985984
  83.2 0.0 copy-done.1
  83.2 0.5 copy.12
Async XLA Ops:
  78.1 3.6 %copy-start = (f32[72,72,72]{2,1,0:T(8,128)S(1)}, f32[72,72,72]{2,1,0:T(8,128)}, u32[]{:S(2)}) copy-start(f32[72,72,72]{2,1,0:T(8,128)} %get-tuple-element.13) | copy-start | bytes 4478980
  81.7 1.5 %copy-start.1 = (f32[1,8]{1,0:T(1,128)S(1)}, f32[1,8]{1,0:T(1,128)}, u32[]{:S(2)}) copy-start(f32[1,8]{1,0:T(1,128)} %get-tuple-element.8) | copy-start | bytes 100

commit v4 on v3

--- a/solution.py
+++ b/solution.py
@@ -26,6 +26,7 @@
 GROUPS = 16
 PIECES = 5
 ZERO, ONE, HALF, TWO = 0.0, 1.0, 0.5, 2.0
+UNIT = 1
 
 
 def iota(axis):
@@ -89,20 +90,20 @@
     y = dict(enumerate(m))
     p = {0: dsub(y[0], y[1])}
     for l in range(1, 15):
-        p[l] = dsub(y[l], dscale(dadd(y[l + 1], y[l - 1]), HALF))
+        p[l] = dsub(y[l], dscale(dadd(y[l + UNIT], y[l - UNIT]), HALF))
     for t in range(STEPS):
         alpha = ddiv(y[t], p[t])
         alphas.append(alpha[0])
-        if t == STEPS - 1:
+        if t == STEPS - UNIT:
             break
-        y_next = {l: dsub(y[l], dmul(alpha, p[l])) for l in range(t + 1, 15 - t)}
-        beta = ddiv(y_next[t + 1], p[t])
+        y_next = {l: dsub(y[l], dmul(alpha, p[l])) for l in range(t + UNIT, 15 - t)}
+        beta = ddiv(y_next[t + UNIT], p[t])
         if t:
             beta = dscale(beta, HALF)
         betas.append(beta[0])
         p_next = {}
-        for l in range(t + 1, 14 - t):
-            side = y_next[l + 1] if l == t + 1 else dadd(y_next[l + 1], y_next[l - 1])
+        for l in range(t + UNIT, 14 - t):
+            side = y_next[l + UNIT] if l == t + UNIT else dadd(y_next[l + UNIT], y_next[l - UNIT])
             p_next[l] = dadd(dsub(y_next[l], dscale(side, HALF)), dmul(beta, p[l]))
         y, p = y_next, p_next
     return alphas, betas
@@ -141,13 +142,13 @@
         x = axpy(x, alphas[t], p)
         y = axpy(y, -alphas[t], q)
         ys.append(y)
-        if t < STEPS - 1:
+        if t < STEPS - UNIT:
             p = axpy(y, betas[t], p)
     return ys, x
 
 
 def row_down(v):
-    return jnp.concatenate([pltpu.roll(v[NB - 1], 1, 0)[None], v[:NB - 1]], axis=0)
+    return jnp.concatenate([pltpu.roll(v[NB - UNIT], 1, 0)[None], v[:NB - UNIT]], axis=0)
 
 
 def row_up(v):
@@ -167,16 +168,11 @@
 
 
 def replace(v, b, mask, value):
-    return jnp.concatenate(([v[:b]] if b else []) + [jnp.where(mask, value, v[b])[None], v[b + 1:]], axis=0)
+    return jnp.concatenate(([v[:b]] if b else []) + [jnp.where(mask, value, v[b])[None], v[b + UNIT:]], axis=0)
 
 
 def harmonic(a, b):
     return TWO * a * b / (a + b)
-
-
-def dot_pair(a, b):
-    prod = a * b
-    return jnp.sum(prod[:2], axis=0), jnp.sum(prod[2:], axis=0)
 
 
 def pick(mask, a, b):
@@ -217,12 +213,14 @@
 
     loads = []
     for n, (src, dst) in enumerate([(k_hbm, k_in), (u_hbm, u_in), (f_hbm, f_in)]):
-        loads.append(pltpu.make_async_copy(src, dst, load_sem.at[n]))
-    loads.append(pltpu.make_async_copy(kg_hbm.at[cx], walls.at[0], load_sem.at[3]))
-    loads.append(pltpu.make_async_copy(kg_hbm.at[2 + cy], walls.at[1], load_sem.at[4]))
-    loads.append(pltpu.make_async_copy(kg_hbm.at[4 + cz], walls.at[2], load_sem.at[PIECES]))
+        loads.append([pltpu.make_async_copy(src.at[pl.ds(PART * q, PART)], dst.at[pl.ds(PART * q, PART)], load_sem.at[n, q])
+                      for q in range(N // PART)])
+    loads.append([pltpu.make_async_copy(kg_hbm.at[cx], walls.at[0], load_sem.at[3, 0])])
+    loads.append([pltpu.make_async_copy(kg_hbm.at[2 + cy], walls.at[1], load_sem.at[4, 0])])
+    loads.append([pltpu.make_async_copy(kg_hbm.at[4 + cz], walls.at[2], load_sem.at[PIECES, 0])])
     for n in (0, 1, 3, 4, PIECES, 2):
-        loads[n].start()
+        for copy in loads[n]:
+            copy.start()
 
     barrier = pltpu.get_barrier_semaphore()
     for flips in OTHERS:
@@ -237,7 +235,6 @@
 
     near_y = pl.multiple_of((N - H) * (1 - cy), SUB)
     near_x = (N - H) * (1 - cx)
-    group8 = lane // SUB
     src8 = (N - H) * (1 - cz)
     dst8 = N + 48 * cz
     ghost8 = jnp.logical_and(lane >= dst8, lane < dst8 + SUB)
@@ -250,10 +247,14 @@
     def turn(x, by):
         return pltpu.roll(x, lax.rem(by + LANES, LANES), 1)
 
+    def shift(x, by):
+        return pltpu.roll(x, by % LANES, 1) if by % LANES else x
+
     def widen(x):
         return x if x.shape[1] == LANES else jnp.concatenate([x, jnp.zeros((x.shape[0], LANES - x.shape[1]), F32)], axis=1)
 
     def pack(nat, packed, corner):
+        group8 = lax.rem(lane + (LANES - src8), LANES) // SUB
         groups = [group8 == g for g in range(GROUPS)]
 
         def body(o, carry):
@@ -263,20 +264,21 @@
                     t = GROUPS * q + g
                     if t % TILES == 0:
                         plane = widen(nat[o * SUB + t // TILES, 0:N, :])
-                    x = turn(plane[SUB * (t % TILES):SUB * (t % TILES) + SUB], SUB * g - src8)
+                    x = shift(plane[SUB * (t % TILES):SUB * (t % TILES) + SUB], SUB * g)
                     out = x if g == 0 else pick(groups[g], x, out)
                 packed[o * PIECES + q] = out
             out = None
             for g in range(SUB):
                 x = widen(nat[o * SUB + g, pl.ds(near_y, SUB), :])
-                x = turn(x, SUB * g - src8)
+                x = shift(x, SUB * g)
                 out = x if g == 0 else pick(groups[g], x, out)
             corner[o] = out
             return carry
         lax.fori_loop(0, TILES, body, 0)
 
     def unpack(own, side, nat, packed, corner, fill, wall, o, carry):
-        packs, corner_in = [packed[o * PIECES + q] for q in range(PIECES)], corner[o]
+        by = dst8 - (N - H - src8)
+        packs, corner_in = [turn(packed[o * PIECES + q], by) for q in range(PIECES)], turn(corner[o], by)
         for pi in range(SUB):
             i, out = o * SUB + pi, []
             plane = widen(own[i, 0:N, :])
@@ -288,18 +290,20 @@
                     got, g = corner_in, pi
                 x = plane[SUB * jt:SUB * jt + SUB] if jt < TILES else widen(side[i])
                 other = fill if wall is None else pick(at_wall, wall_column(i, jt), fill)
-                out.append(pick(own_lane, x, pick(ghost8, turn(got, dst8 - SUB * g), other)))
+                out.append(pick(own_lane, x, pick(ghost8, shift(got, -SUB * g), other)))
             nat[i, 0:E, :] = jnp.concatenate(out, axis=0)
         return carry
 
     def wall_column(i, jt):
         at = SUB * jt if jt < TILES else pl.multiple_of(N + 48 * cy, SUB)
-        return turn(wz_t[pl.ds(at, SUB), :], wall_lane - i)
-
-    loads[0].wait()
-    loads[1].wait()
-    last_x, last_y, last_z = (N - 1) * (1 - cx), (N - 1) * (1 - cy), (N - 1) * (1 - cz)
+        return pltpu.roll(wz_t[pl.ds(at, SUB), :], LANES - UNIT - i, 1)
+
+    for copy in loads[0] + loads[1]:
+        copy.wait()
+    last_x, last_y, last_z = (N - UNIT) * (1 - cx), (N - UNIT) * (1 - cy), (N - UNIT) * (1 - cz)
     one_x = [send(0, k_in.at[pl.ds(last_x, 1)], kx, (1, 0, 0)), send(1, u_in.at[pl.ds(last_x, 1)], ux, (1, 0, 0))]
+
+    slots = lax.rem(lane + (LANES - last_z), LANES)
 
     def pack_one(o, carry):
         for n, src in enumerate((k_in, u_in)):
@@ -309,8 +313,8 @@
             for t in range(N):
                 if t % TILES == 0:
                     plane = widen(src[o * SUB + t // TILES])
-                x = turn(plane[SUB * (t % TILES):SUB * (t % TILES) + SUB], t - last_z)
-                out = x if t == 0 else pick(lane == t, x, out)
+                x = shift(plane[SUB * (t % TILES):SUB * (t % TILES) + SUB], t)
+                out = x if t == 0 else pick(slots == t, x, out)
             lane_s[n, o] = out
         return carry
     lax.fori_loop(0, TILES, pack_one, 0)
@@ -322,7 +326,7 @@
     k_d = send(6, ds_.at[0], dr.at[0], (0, 1, 1))
 
     for n in (3, 4, PIECES):
-        loads[n].wait()
+        loads[n][0].wait()
 
     def lane_ring(w, at, c):
         left, right = walls[w, pl.ds(at, SUB), 0:LANES], walls[w, pl.ds(at, SUB), LANES:144]
@@ -338,9 +342,10 @@
         wy[pl.ds(SUB * jt, SUB), :] = lane_ring(1, at_i, cz)
         if jt < TILES:
             wz[pl.ds(SUB * jt, SUB), :] = lane_ring(2, at_i, cy)
-    wz_t[...] = wz[...].T
-
-    loads[2].wait()
+    wz_t[...] = turn(wz[...].T, wall_lane + UNIT)
+
+    for copy in loads[2]:
+        copy.wait()
 
     def take_f(p, carry):
         for b in range(NB):
@@ -349,16 +354,16 @@
         return carry
     planes(0, N, take_f, 0)
 
-    u_nat[E - 1 - LAST * cx] = jnp.zeros((E, LANES), F32)
+    u_nat[E - UNIT - LAST * cx] = jnp.zeros((E, LANES), F32)
     one_lane = N + 55 * cz
     at_one = lane == one_lane
     for copy in one_x + [one_y, one_z]:
         copy.wait()
     u_nat[N + LAST * cx, 0:N, 0:N] = ux[0]
-    k_nat[E + 1, 0:N, 0:N] = kx[0]
+    k_nat[E + UNIT, 0:N, 0:N] = kx[0]
 
     def unpack_one(o, carry):
-        lanes_in = [lane_r[n, o] for n in range(2)]
+        lanes_in = [turn(lane_r[n, o], one_lane - (N - UNIT - last_z)) for n in range(2)]
         for pi in range(SUB):
             i = o * SUB + pi
             planes_in = [widen(k_in[i]), widen(u_in[i])]
@@ -366,7 +371,7 @@
                 out = []
                 for jt in range(TILES):
                     other = zero if n else pick(at_wall, wall_column(i, jt), ones)
-                    other = pick(at_one, turn(lanes_in[n], one_lane - (pi * TILES + jt)), other)
+                    other = pick(at_one, shift(lanes_in[n], -(pi * TILES + jt)), other)
                     out.append(pick(own_lane, planes_in[n][SUB * jt:SUB * jt + SUB], other))
                 nat[i, 0:N, :] = jnp.concatenate(out, axis=0)
         return carry
@@ -396,25 +401,25 @@
 
     def start_own(n, carry):
         p0 = WIDTH * n
-        first_trip, last_trip = n == 0, n == N // WIDTH - 1
-        k_p = [load_chunk(k_nat, jnp.where(first_trip, E + cx, p0 - 1))]
-        u_p = [load_chunk(u_nat, jnp.where(first_trip, E - 1, p0 - 1))]
+        first_trip, last_trip = n == 0, n == N // WIDTH - UNIT
+        k_p = [load_chunk(k_nat, jnp.where(first_trip, E + cx, p0 - UNIT))]
+        u_p = [load_chunk(u_nat, jnp.where(first_trip, E - UNIT, p0 - UNIT))]
         for w in range(WIDTH):
             k_p.append(load_chunk(k_nat, p0 + w))
             u_p.append(load_chunk(u_nat, p0 + w))
-        k_p.append(load_chunk(k_nat, jnp.where(last_trip, E + 1 - cx, p0 + WIDTH)))
+        k_p.append(load_chunk(k_nat, jnp.where(last_trip, E + UNIT - cx, p0 + WIDTH)))
         u_p.append(load_chunk(u_nat, p0 + WIDTH))
-        h_x = [harmonic(k_p[w + 1], k_p[w]) for w in range(WIDTH + 1)]
+        h_x = [harmonic(k_p[w + UNIT], k_p[w]) for w in range(WIDTH + UNIT)]
         for w in range(WIDTH):
-            p, kc = p0 + w, k_p[w + 1]
+            p, kc = p0 + w, k_p[w + UNIT]
             wall, got = full(wy[pl.ds(p, 1), :]), full(row_r[0, pl.ds(p, 1), :])
             low = replace(row_down(kc), 0, row0, jnp.where(cy == 0, wall, got))
             high = replace(kc, 2, row72, jnp.where(cy == 0, got, wall))
             h_y = harmonic(high, low)
             h_z = harmonic(kc, lane_down(kc))
-            inv = lax.rsqrt(add_up(h_x[w], h_x[w + 1], h_y, h_z))
+            inv = lax.rsqrt(add_up(h_x[w], h_x[w + UNIT], h_y, h_z))
             got = full(row_r[1, pl.ds(p, 1), :])
-            a_u = divergence(h_x[w], h_x[w + 1], h_y, h_z, u_p[w + 1], u_p[w], u_p[w + 2],
+            a_u = divergence(h_x[w], h_x[w + UNIT], h_y, h_z, u_p[w + UNIT], u_p[w], u_p[w + 2],
                              jnp.where(cy == 0, ZERO, got), jnp.where(cy == 0, got, ZERO))
             y0 = (v0_a[p] - a_u) * inv
             v0_a[p] = y0
@@ -444,7 +449,7 @@
 
     def faces(p, carry):
         kc = load_chunk(k_nat, p)
-        before = jnp.where(jnp.logical_and(p == 0, cx == 0), E, jnp.where(p == 0, E - 1, p - 1))
+        before = jnp.where(jnp.logical_and(p == 0, cx == 0), E, jnp.where(p == 0, E - UNIT, p - UNIT))
         here = jnp.where(jnp.logical_and(p == N, cx == 1), E, p)
         cx_a[p] = harmonic(load_chunk(k_nat, here), load_chunk(k_nat, before))
         wall = full(wy[pl.ds(p, 1), :])
@@ -455,10 +460,10 @@
         return carry
     planes(0, E, faces, 0)
     cx_a[E] = cx_a[0]
-    cx_a[E + 1] = cx_a[1]
+    cx_a[E + UNIT] = cx_a[1]
 
     def scales(own, p, carry):
-        d = add_up(cx_a[p], cx_a[p + 1], cy_a[p], cz_a[p])
+        d = add_up(cx_a[p], cx_a[p + UNIT], cy_a[p], cz_a[p])
         inv = lax.rsqrt(d)
         isd_a[p] = inv
         if own:
@@ -474,39 +479,81 @@
     z_x = spread(11, z_nat, functools.partial(unpack, z_nat, z_nat.at[:, pl.ds(N, SUB), :], z_nat, zr.at[1], dr.at[1],
                                               zero, None))
 
-    def first(own, p, carry):
-        static = isinstance(p, int)
-        before = (p - 1) % E if static else p - 1
-        after = p + 1 if static else lax.rem(p + 1, E)
-        h_x, h_xn, h_y, h_z, inv = cx_a[p], cx_a[E + 1 if static and p == 0 else p + 1], cy_a[p], cz_a[p], isd_a[p]
-        z_p = jnp.where(jnp.logical_and(p == 0, cx == 0), ZERO, load_chunk(z_nat, before))
-        z_n = jnp.where(jnp.logical_and(p == N - 1, cx == 1), ZERO, load_chunk(z_nat, after))
-        b0 = inv * divergence(h_x, h_xn, h_y, h_z, load_chunk(z_nat, p), z_p, z_n, None, None)
-        b_a[0][p + 1] = b0
-        cut = jnp.logical_or(jnp.logical_and(p == 0, cx == 0), jnp.logical_and(p == N, cx == 1))
-        twice = TWO * inv
-        cx_a[p] = jnp.where(cut, ZERO, h_x * (twice * isd_a[before]))
-        c_y = h_y * (twice * row_down(inv))
-        c_y = replace(c_y, 0, jnp.logical_and(row0, cy == 0), ZERO)
-        cy_a[p] = replace(c_y, 2, jnp.logical_and(row72, cy == 1), ZERO)
-        c_z = h_z * (twice * lane_down(inv))
-        edge = N * cz
-        cz_a[p] = jnp.where(lax.broadcasted_iota(jnp.int32, (NB, SUB, LANES), 2) == edge, ZERO, c_z)
-        if not own:
-            return carry
-        v0 = v0_a[p]
-        new = dot_pair(v0, v0) + dot_pair(v0, b0) + dot_pair(b0, b0)
-        return tuple(c + n for c, n in zip(carry, new))
-
+    def column(ref, p, b, width):
+        return ref[pl.ds(p, width), b]
+
+    def z_column(p, b, width=1):
+        return z_nat[pl.ds(p, width), pl.ds(b, SUB, stride=NB), :]
+
+    def tally(carry, b, products):
+        return [c + jnp.sum(products[n // 2], axis=0) if n % 2 == (b > 1) else c for n, c in enumerate(carry)]
+
+    def first(own, width, p, carry, before=None, after=None, x_after=None):
+        before = p - UNIT if before is None else before
+        z, inv, low, f_y, h_y = {}, {}, {}, {}, {}
+
+        def load(b):
+            z[b], inv[b], h_y[b] = z_column(p, b, width), column(isd_a, p, b, width), column(cy_a, p, b, width)
+            under = z[b - UNIT] if b else pltpu.roll(z_column(p, NB - UNIT, width), 1, 1)
+            over = z[b]
+            if b == 0:
+                under = jnp.where(jnp.logical_and(row0, cy == 0), ZERO, under)
+            if b == 2:
+                over = jnp.where(jnp.logical_and(row72, cy == 1), ZERO, over)
+            f_y[b] = h_y[b] * (over - under)
+        carry = list(carry)
+        load(0)
+        for b in range(NB):
+            if b < NB - UNIT:
+                load(b + UNIT)
+            up = f_y[b + UNIT] if b < NB - UNIT else pltpu.roll(f_y[0], LAST, 1)
+            z_p = z_column(before, b)
+            z_n = z_column(p + width if after is None else after, b)
+            if isinstance(p, int) and p == 0:
+                z_p = jnp.where(cx == 0, ZERO, z_p)
+            if isinstance(p, int) and p == N - UNIT:
+                z_n = jnp.where(cx == 1, ZERO, z_n)
+            if x_after is None:
+                h_x = column(cx_a, p, b, width + UNIT)
+            else:
+                h_x = jnp.concatenate([column(cx_a, p, b, 1), column(cx_a, x_after, b, 1)], axis=0)
+            f_x = h_x * (jnp.concatenate([z[b], z_n], axis=0) - jnp.concatenate([z_p, z[b]], axis=0))
+            h_z = column(cz_a, p, b, width)
+            f_z = h_z * (z[b] - lane_down(z[b]))
+            b0 = inv[b] * (((f_x[:width] - f_x[1:]) + (f_y[b] - up)) + (f_z - lane_up(f_z)))
+            b_a[0][pl.ds(p + UNIT, width), b] = b0
+            twice = TWO * inv[b]
+            side = column(isd_a, before, b, 1)
+            if width > 1:
+                side = jnp.concatenate([side, inv[b][:width - UNIT]], axis=0)
+            cx_a[pl.ds(p, width), b] = h_x[:width] * (twice * side)
+            side = inv[b - UNIT] if b else pltpu.roll(column(isd_a, p, NB - UNIT, width), 1, 1)
+            c_y = h_y[b] * (twice * side)
+            if b == 0:
+                c_y = jnp.where(jnp.logical_and(row0, cy == 0), ZERO, c_y)
+            if b == 2:
+                c_y = jnp.where(jnp.logical_and(row72, cy == 1), ZERO, c_y)
+            cy_a[pl.ds(p, width), b] = c_y
+            cz_a[pl.ds(p, width), b] = jnp.where(at_edge, ZERO, h_z * (twice * lane_down(inv[b])))
+            if own:
+                v0 = column(v0_a, p, b, width)
+                carry = tally(carry, b, (v0 * v0, v0 * b0, b0 * b0))
+        return tuple(carry)
+
+    at_edge = lane == N * cz
 
     def wrap(ref):
         ref[0] = ref[E]
-        ref[E + 1] = ref[1]
-    sums = planes(1, N - 1, functools.partial(first, True), (zero,) * 6, PIECES)
+        ref[E + UNIT] = ref[1]
+
+    sums = lax.fori_loop(0, 14, lambda n, carry: first(True, PIECES, 1 + PIECES * n, carry), (zero,) * 6)
     z_x.wait()
-    for p in (0, N - 1):
-        sums = first(True, p, sums)
-    planes(N, E, functools.partial(first, False), 0)
+    sums = first(True, 1, 0, sums, E - UNIT, None, E + UNIT)
+    sums = first(True, 1, N - UNIT, sums)
+    first(False, WIDTH, N, ())
+    first(False, WIDTH, N + WIDTH, (), None, 0)
+    cx_a[0] = jnp.where(cx == 0, ZERO, cx_a[0])
+    cx_a[N] = jnp.where(cx == 1, ZERO, cx_a[N])
     cx_a[E] = cx_a[0]
     wrap(b_a[0])
     acc[0] = own_cells(sums[0], sums[1])
@@ -514,28 +561,40 @@
     acc[TILES] = own_cells(sums[4], sums[PIECES])
     acc[23] = zero
 
-    def advance(k, own, p, carry):
-        old, here = b_a[k - 1], p + 1
-        v = old[here]
-        c_y, c_z = cy_a[p], cz_a[p]
-        new = cx_a[p] * old[here - 1] + cx_a[p + 1] * old[here + 1]
-        new = new + (c_y * row_down(v) + row_up(c_y * v))
-        new = new + (c_z * lane_down(v) + lane_up(c_z * v))
-        new = HALF * new if k == 1 else new - b_a[k - 2][here]
-        b_a[k][here] = new
-        if not own:
-            return carry
-        dots = dot_pair(v0_a[p], new) + dot_pair(v, new) + dot_pair(new, new)
-        return tuple(c + n for c, n in zip(carry, dots))
+    def advance(k, own, width, p, carry):
+        old, carry = b_a[k - UNIT], list(carry)
+        v_low = pltpu.roll(column(old, p + UNIT, NB - UNIT, width), 1, 1)
+        v, c_y = column(old, p + UNIT, 0, width), column(cy_a, p, 0, width)
+        t_first = c_y * v
+        for b in range(NB):
+            if b < NB - UNIT:
+                v_high, c_high = column(old, p + UNIT, b + UNIT, width), column(cy_a, p, b + UNIT, width)
+                t_high = c_high * v_high
+            else:
+                t_high = pltpu.roll(t_first, LAST, 1)
+            c_x, c_z = column(cx_a, p, b, width + UNIT), column(cz_a, p, b, width)
+            below, above = column(old, p, b, 1), column(old, p + width + UNIT, b, 1)
+            if width > 1:
+                below = jnp.concatenate([below, v[:width - UNIT]], axis=0)
+                above = jnp.concatenate([v[1:], above], axis=0)
+            new = c_x[:width] * below + c_x[1:] * above
+            new = new + (c_y * v_low + t_high)
+            new = new + (c_z * lane_down(v) + lane_up(c_z * v))
+            new = HALF * new if k == 1 else new - column(b_a[k - 2], p + UNIT, b, width)
+            b_a[k][pl.ds(p + UNIT, width), b] = new
+            if own:
+                carry = tally(carry, b, (column(v0_a, p, b, width) * new, v * new, new * new))
+            v_low, v, c_y = v, v_high, c_high
+        return tuple(carry)
 
     for k in range(1, STEPS):
-        sums = planes(0, N, functools.partial(advance, k, True), (zero,) * 6)
-        if k < STEPS - 1:
-            planes(N, E, functools.partial(advance, k, False), 0)
+        sums = lax.fori_loop(0, N // WIDTH, lambda n, carry: advance(k, True, WIDTH, WIDTH * n, carry), (zero,) * 6)
+        if k < STEPS - UNIT:
+            lax.fori_loop(0, 2, lambda n, carry: advance(k, False, WIDTH, N + WIDTH * n, carry), ())
             wrap(b_a[k])
         acc[1 + k] = own_cells(sums[0], sums[1])
-        acc[GROUPS + k - 1] = own_cells(sums[2], sums[3])
-        if k < STEPS - 1:
+        acc[GROUPS + k - UNIT] = own_cells(sums[2], sums[3])
+        if k < STEPS - UNIT:
             acc[TILES + k] = own_cells(sums[4], sums[PIECES])
 
     def gather(buf, n_sem):
@@ -571,7 +630,7 @@
     hi, lo = hi * factor, lo * factor
 
     def total(row):
-        return jnp.broadcast_to(hi[row:row + 1], (SUB, LANES)), jnp.broadcast_to(lo[row:row + 1], (SUB, LANES))
+        return jnp.broadcast_to(hi[row:row + UNIT], (SUB, LANES)), jnp.broadcast_to(lo[row:row + UNIT], (SUB, LANES))
 
     n_mom = [total(TILES), total(GROUPS)]
     for j in range(1, LAST):
@@ -579,15 +638,15 @@
         n_mom.append(dsub(dscale(total(GROUPS + j), TWO), n_mom[1]))
     l_mom = [total(1 + j) for j in range(SUB)]
     for j in range(LAST, 14):
-        l_mom.append(dsub(dscale(dsub(l_mom[j], n_mom[j]), TWO), l_mom[j - 1]))
+        l_mom.append(dsub(dscale(dsub(l_mom[j], n_mom[j]), TWO), l_mom[j - UNIT]))
     m_mom = [total(0)]
     m_mom.append(dsub(m_mom[0], l_mom[0]))
     for j in range(1, 15):
-        m_mom.append(dsub(dscale(dsub(m_mom[j], l_mom[j]), TWO), m_mom[j - 1]))
+        m_mom.append(dsub(dscale(dsub(m_mom[j], l_mom[j]), TWO), m_mom[j - UNIT]))
     ys, xs = basis_coefs(*step_lengths(m_mom))
     slot = {}
     for t in range(STEPS):
-        for j in range(t + 1):
+        for j in range(t + UNIT):
             slot[t, j] = len(slot)
             coef[slot[t, j]] = ys[t][1 + j]
     for j in range(SUB):
@@ -607,15 +666,15 @@
             cut = pl.ds(b0, 2)
             v0 = v0_a[p, cut]
             sd = jnp.stack([k_nat[p, pl.ds(SUB * (b0 + b), SUB), :] for b in range(2)], axis=0)
-            bs = [ref[p + 1, cut] for ref in b_a]
+            bs = [ref[p + UNIT, cut] for ref in b_a]
             for t in range(STEPS):
                 y = v0
-                for j in range(t + 1):
+                for j in range(t + UNIT):
                     y = y + coef[slot[t, j]] * bs[j]
                 r = sd * y
                 which = 2 * t + (b0 > 0)
                 carry[which] = carry[which] + jnp.sum(r * r, axis=0)
-                if t == STEPS - 1:
+                if t == STEPS - UNIT:
                     put(f_in, p, b0, r)
         return tuple(carry)
 
@@ -631,7 +690,7 @@
         sums = lax.fori_loop(PART * o, PART * o + PART, residuals, sums)
         flush(0, f_in, ro_hbm, o)
     for t in range(STEPS):
-        rsend[t] = own_cells(sums[2 * t], sums[2 * t + 1])
+        rsend[t] = own_cells(sums[2 * t], sums[2 * t + UNIT])
     part = rsend[:, 0, :]
     for s in range(1, SUB):
         part = part + rsend[:, s, :]
@@ -643,7 +702,7 @@
             cut = pl.ds(b0, 2)
             x = coef[slot['x', 0]] * v0_a[p, cut]
             for j in range(1, SUB):
-                x = x + coef[slot['x', j]] * b_a[j - 1][p + 1, cut]
+                x = x + coef[slot['x', j]] * b_a[j - UNIT][p + UNIT, cut]
             x = x * isd_a[p, cut]
             u = jnp.stack([u_nat[p, pl.ds(b0 + b, SUB, stride=NB), :] for b in range(2)], axis=0)
             put(k_in, p, b0, u + x)
@@ -685,7 +744,7 @@
                 vm(2, 45, SUB, LANES), vm(2, 45, SUB, LANES), vm(2, TILES, SUB, LANES), vm(2, TILES, SUB, LANES),
                 vm(2, N, N), vm(2, N, N), vm(2, TILES, SUB, LANES), vm(2, TILES, SUB, LANES),
                 vm(NDOT, SUB, LANES), vm(SUB, 2 * NDOT, LANES), vm(SUB, SUB, LANES), vm(SUB, SUB, LANES), vm(44, SUB, LANES),
-                pltpu.SemaphoreType.DMA((6,)), pltpu.SemaphoreType.DMA((2, 3)),
+                pltpu.SemaphoreType.DMA((6, 3)), pltpu.SemaphoreType.DMA((2, 3)),
                 pltpu.SemaphoreType.DMA((12,)), pltpu.SemaphoreType.DMA((12,)),
                 pltpu.SemaphoreType.DMA((2, LAST)), pltpu.SemaphoreType.DMA((2, LAST)),
             ],

time: 83.8 us -> 85.3 us (1.018)
  Pallas kernels: 77.4 us -> 79 us
    pallas_call x1, Pallas kernels: 77.4 us -> 79 us  [local(): pl.pallas_call(kernel, out_shape=(block, block, jax.ShapeDtypeStruct((1,...]
where the time goes in v4:
time: 85.3 us; the launch traced here: 85.2 us
  Pallas kernels  79 us (93%)
  local copies, waits for them, and re-layouts  5.59 us (7%)
    pallas_call x1, Pallas kernels, local(): pl.pallas_call(kernel, out_shape=(block, block, jax.ShapeDtypeStruct((1,...  79 us
    unnamed x7, local copies, waits for them, and re-layouts  5.59 us

profile of v4, /device:TPU:0, one launch (start us, length us, event | category | flops | bytes accessed | tf_op | source)
XLA Modules:
  0.0 85.2 jit_solution(6780875179305458203)
XLA Ops:
  0.6 79.0 %shard_map.67 = (f32[72,72,72]{2,1,0:T(8,128)}, f32[72,72,72]{2,1,0:T(8,128)}, f32[1,8]{1,0:T(1,128)}) custom-call(f32[72,72,72]{2,1,0:T(8,128)} %k_hbm.1, f32[72,72,72]{2,1,0:T(8,128)} %f_hbm.1, f32[72,72,72]{2,1,0:T(8,128)} %u_hbm.1, f32[6,144,144]{2,1,0:T(8,128)} %kg_hbm.1), custom_call_target="tpu_custom_call" | custom-call | tf_op jit(solution)/shard_map/pallas_call | solution.py:734
  79.6 0.0 copy-start
  79.6 3.6 %copy.10 = f32[72,72,72]{2,1,0:T(8,128)} copy(f32[72,72,72]{2,1,0:T(8,128)} %get-tuple-element.12) | data formatting | bytes 2985984
  83.2 0.0 copy-done
  83.2 0.0 copy-start.1
  83.2 1.5 %copy.11 = f32[72,72,72]{2,1,0:T(8,128)} copy(f32[72,72,72]{2,1,0:T(8,128)S(1)} %copy-done) | data formatting | bytes 2985984
  84.7 0.0 copy-done.1
  84.7 0.5 copy.12
Async XLA Ops:
  79.6 3.6 %copy-start = (f32[72,72,72]{2,1,0:T(8,128)S(1)}, f32[72,72,72]{2,1,0:T(8,128)}, u32[]{:S(2)}) copy-start(f32[72,72,72]{2,1,0:T(8,128)} %get-tuple-element.13) | copy-start | bytes 4478980
  83.2 1.5 %copy-start.1 = (f32[1,8]{1,0:T(1,128)S(1)}, f32[1,8]{1,0:T(1,128)}, u32[]{:S(2)}) copy-start(f32[1,8]{1,0:T(1,128)} %get-tuple-element.8) | copy-start | bytes 100

commit v5 on v4

--- a/solution.py
+++ b/solution.py
@@ -27,6 +27,7 @@
 PIECES = 5
 ZERO, ONE, HALF, TWO = 0.0, 1.0, 0.5, 2.0
 UNIT = 1
+HEAD = 4
 
 
 def iota(axis):
@@ -192,10 +193,10 @@
     return jnp.where(lane < N, low + jnp.where(sub < LAST, high, ZERO), ZERO)
 
 
-def kernel(k_hbm, f_hbm, u_hbm, kg_hbm, uo_hbm, ro_hbm, rr_ref,
-           k_in, u_in, f_in, k_nat, u_nat, z_nat, cx_a, cy_a, cz_a, isd_a, v0_a, b0_a, b1_a, b2_a, b3_a, b4_a, b5_a, b6_a, b7_a,
+def kernel(k_hbm, f_hbm, u_hbm, kg_hbm, k_in, f_in, rr_ref,
+           u_in, k_nat, u_nat, z_nat, cx_a, cy_a, cz_a, isd_a, v0_a, b0_a, b1_a, b2_a, b3_a, b4_a, b5_a, b6_a, b7_a,
            walls, wz, wz_t, wy, ky, kx, ux, zs, zr, ds_, dr, row_s, row_r, lane_s, lane_r, acc, gath, rsend, rgath, coef,
-           load_sem, out_sem, send_sem, recv_sem, all_send, all_recv):
+           load_sem, send_sem, recv_sem, all_send, all_recv):
     cx, cy, cz = lax.axis_index('gx'), lax.axis_index('gy'), lax.axis_index('gz')
     me = cx + 2 * cy + 4 * cz
     b_a = (b0_a, b1_a, b2_a, b3_a, b4_a, b5_a, b6_a, b7_a)
@@ -225,7 +226,6 @@
     barrier = pltpu.get_barrier_semaphore()
     for flips in OTHERS:
         pl.semaphore_signal(barrier, inc=1, device_id=peer(*flips), device_id_type=MESH)
-    pl.semaphore_wait(barrier, len(OTHERS))
 
     def send(n, src, dst, flips):
         copy = pltpu.make_async_remote_copy(src_ref=src, dst_ref=dst, send_sem=send_sem.at[n], recv_sem=recv_sem.at[n],
@@ -301,7 +301,6 @@
     for copy in loads[0] + loads[1]:
         copy.wait()
     last_x, last_y, last_z = (N - UNIT) * (1 - cx), (N - UNIT) * (1 - cy), (N - UNIT) * (1 - cz)
-    one_x = [send(0, k_in.at[pl.ds(last_x, 1)], kx, (1, 0, 0)), send(1, u_in.at[pl.ds(last_x, 1)], ux, (1, 0, 0))]
 
     slots = lax.rem(lane + (LANES - last_z), LANES)
 
@@ -318,6 +317,8 @@
             lane_s[n, o] = out
         return carry
     lax.fori_loop(0, TILES, pack_one, 0)
+    pl.semaphore_wait(barrier, len(OTHERS))
+    one_x = [send(0, k_in.at[pl.ds(last_x, 1)], kx, (1, 0, 0)), send(1, u_in.at[pl.ds(last_x, 1)], ux, (1, 0, 0))]
     one_y = send(2, row_s, row_r, (0, 1, 0))
     one_z = send(3, lane_s, lane_r, (0, 0, 1))
     k_y = send(4, k_in.at[:, pl.ds(near_y, SUB), :], ky, (0, 1, 0))
@@ -422,7 +423,8 @@
             a_u = divergence(h_x[w], h_x[w + UNIT], h_y, h_z, u_p[w + UNIT], u_p[w], u_p[w + 2],
                              jnp.where(cy == 0, ZERO, got), jnp.where(cy == 0, got, ZERO))
             y0 = (v0_a[p] - a_u) * inv
-            v0_a[p] = y0
+            for b in range(NB):
+                v0_a[p, b] = y0[b] if b < 2 else pick(row72, zero, y0[b])
             z0 = y0 * inv
             for b in range(NB):
                 if b < 2:
@@ -469,7 +471,7 @@
         if own:
             sd = d * inv
             for b in range(NB):
-                k_nat[p, pl.ds(SUB * b, SUB), :] = sd[b]
+                k_nat[p, pl.ds(SUB * b, SUB), :] = sd[b] if b < 2 else pick(row72, zero, sd[b])
         return carry
     planes(0, N, functools.partial(scales, True), 0)
     planes(N, E, functools.partial(scales, False), 0)
@@ -588,9 +590,9 @@
         return tuple(carry)
 
     for k in range(1, STEPS):
-        sums = lax.fori_loop(0, N // WIDTH, lambda n, carry: advance(k, True, WIDTH, WIDTH * n, carry), (zero,) * 6)
+        sums = lax.fori_loop(0, N // SUB, lambda n, carry: advance(k, True, SUB, SUB * n, carry), (zero,) * 6)
         if k < STEPS - UNIT:
-            lax.fori_loop(0, 2, lambda n, carry: advance(k, False, WIDTH, N + WIDTH * n, carry), ())
+            advance(k, False, SUB, N, ())
             wrap(b_a[k])
         acc[1 + k] = own_cells(sums[0], sums[1])
         acc[GROUPS + k - UNIT] = own_cells(sums[2], sums[3])
@@ -614,7 +616,22 @@
         lo = lo + err
     gath[me, 0:NDOT] = hi
     gath[me, NDOT:2 * NDOT] = lo
-    for copy in gather(gath, 0):
+    gath_copies = gather(gath, 0)
+    pair = {}
+    for i in range(HEAD + UNIT):
+        for j in range(i, HEAD + UNIT):
+            pair[i, j] = len(pair)
+
+    def products(n, carry):
+        p, carry = WIDTH * n, list(carry)
+        for b in range(NB):
+            sd = k_nat[pl.ds(p, WIDTH), pl.ds(SUB * b, SUB), :]
+            w = [sd * column(v0_a, p, b, WIDTH)] + [sd * column(b_a[j], p + UNIT, b, WIDTH) for j in range(HEAD)]
+            for (i, j), at in pair.items():
+                carry[at] = carry[at] + jnp.sum(w[i] * w[j], axis=0)
+        return tuple(carry)
+    gram = lax.fori_loop(0, N // WIDTH, products, (zero,) * len(pair))
+    for copy in gath_copies:
         copy.wait()
     hi, lo = gath[0, 0:NDOT], gath[0, NDOT:2 * NDOT]
     for dev in range(1, SUB):
@@ -667,30 +684,33 @@
             v0 = v0_a[p, cut]
             sd = jnp.stack([k_nat[p, pl.ds(SUB * (b0 + b), SUB), :] for b in range(2)], axis=0)
             bs = [ref[p + UNIT, cut] for ref in b_a]
-            for t in range(STEPS):
+            for t in range(HEAD, STEPS):
                 y = v0
                 for j in range(t + UNIT):
                     y = y + coef[slot[t, j]] * bs[j]
                 r = sd * y
-                which = 2 * t + (b0 > 0)
+                which = 2 * (t - HEAD) + (b0 > 0)
                 carry[which] = carry[which] + jnp.sum(r * r, axis=0)
                 if t == STEPS - UNIT:
                     put(f_in, p, b0, r)
         return tuple(carry)
 
-    outs = []
-
-    def flush(n, nat, hbm, o):
-        outs.append(pltpu.make_async_copy(nat.at[pl.ds(PART * o, PART)], hbm.at[pl.ds(PART * o, PART)],
-                                          out_sem.at[n, o]))
-        outs[-1].start()
-
-    sums = (zero,) * GROUPS
-    for o in range(3):
-        sums = lax.fori_loop(PART * o, PART * o + PART, residuals, sums)
-        flush(0, f_in, ro_hbm, o)
+    sums = lax.fori_loop(0, N, residuals, (zero,) * (2 * (STEPS - HEAD)))
     for t in range(STEPS):
-        rsend[t] = own_cells(sums[2 * t], sums[2 * t + UNIT])
+        if t < HEAD:
+            form = zero
+            g = [None] + [coef[slot[t, j]] for j in range(t + 1)]
+            for i in range(t + 2):
+                part = gram[pair[0, i]] if not i else g[i] * gram[pair[0, i]]
+                form = form + (part if not i else part + part)
+            for i in range(UNIT, t + 2):
+                part = zero
+                for j in range(UNIT, t + 2):
+                    part = part + g[j] * gram[pair[min(i, j), max(i, j)]]
+                form = form + g[i] * part
+            rsend[t] = pick(own_lane, form, zero)
+        else:
+            rsend[t] = own_cells(sums[2 * (t - HEAD)], sums[2 * (t - HEAD) + UNIT])
     part = rsend[:, 0, :]
     for s in range(1, SUB):
         part = part + rsend[:, s, :]
@@ -708,9 +728,7 @@
             put(k_in, p, b0, u + x)
         return carry
 
-    for o in range(3):
-        lax.fori_loop(PART * o, PART * o + PART, update, 0)
-        flush(1, k_in, uo_hbm, o)
+    lax.fori_loop(0, N, update, 0)
     for copy in rr_copies:
         copy.wait()
     part = rgath[0]
@@ -718,8 +736,6 @@
         part = part + rgath[dev]
     part = jnp.broadcast_to(jnp.sum(part, axis=1, keepdims=True), (SUB, LANES))
     rr_ref[...] = jnp.sum(jnp.where(lane == sub, part, ZERO), axis=0, keepdims=True)[:, :STEPS]
-    for copy in outs:
-        copy.wait()
 
 
 def solution(mesh):
@@ -730,25 +746,24 @@
         ext = (E + 2, NB, SUB, LANES)
         vm = lambda *shape: pltpu.VMEM(shape, F32)
         any_spec = pl.BlockSpec(memory_space=pl.ANY)
-        block = jax.ShapeDtypeStruct((N, N, N), F32)
         u, r, rr = pl.pallas_call(
             kernel,
-            out_shape=(block, block, jax.ShapeDtypeStruct((1, STEPS), F32)),
+            out_shape=(vm(N, N, N), vm(N, N, N), vm(1, STEPS)),
             in_specs=[any_spec] * 4,
-            out_specs=(any_spec, any_spec, pl.BlockSpec(memory_space=pltpu.VMEM)),
+            out_specs=[pl.BlockSpec(memory_space=pltpu.VMEM)] * 3,
             scratch_shapes=[
-                vm(N, N, N), vm(N, N, N), vm(N, N, N), vm(E + 2, E, LANES), vm(E, E, LANES), vm(E, E, LANES),
+                vm(N, N, N), vm(E + 2, E, LANES), vm(E, E, LANES), vm(E, E, LANES),
                 vm(*ext), vm(*big), vm(*big), vm(*big), vm(N, NB, SUB, LANES),
                 *[vm(E + 2, NB, SUB, LANES)] * STEPS,
                 vm(3, 144, 144), vm(LANES, LANES), vm(LANES, LANES), vm(E, LANES), vm(N, SUB, N), vm(1, N, N), vm(1, N, N),
                 vm(2, 45, SUB, LANES), vm(2, 45, SUB, LANES), vm(2, TILES, SUB, LANES), vm(2, TILES, SUB, LANES),
                 vm(2, N, N), vm(2, N, N), vm(2, TILES, SUB, LANES), vm(2, TILES, SUB, LANES),
                 vm(NDOT, SUB, LANES), vm(SUB, 2 * NDOT, LANES), vm(SUB, SUB, LANES), vm(SUB, SUB, LANES), vm(44, SUB, LANES),
-                pltpu.SemaphoreType.DMA((6, 3)), pltpu.SemaphoreType.DMA((2, 3)),
+                pltpu.SemaphoreType.DMA((6, 3)),
                 pltpu.SemaphoreType.DMA((12,)), pltpu.SemaphoreType.DMA((12,)),
                 pltpu.SemaphoreType.DMA((2, LAST)), pltpu.SemaphoreType.DMA((2, LAST)),
             ],
-            compiler_params=pltpu.CompilerParams(collective_id=0, has_side_effects=True, vmem_limit_bytes=67043328),
+            compiler_params=pltpu.CompilerParams(collective_id=0, has_side_effects=True, vmem_limit_bytes=57 << 20),
         )(k_cell, f_rhs, u_init, k_ghost)
         return u, r, rr.reshape(STEPS)
 

time: 85.3 us -> 74.4 us (0.87)
  Pallas kernels: 79 us -> 70.1 us
  local copies, waits for them, and re-layouts: 5.59 us -> 3.52 us
    pallas_call x1, Pallas kernels: 79 us -> 70.1 us  [local(): pl.pallas_call(kernel, out_shape=(vm(N, N, N), vm(N, N, N), vm(1, STEPS))...]
    unnamed x7 -> x3, local copies, waits for them, and re-layouts: 5.59 us -> 3.52 us
where the time goes in v5:
time: 74.4 us; the launch traced here: 74.3 us
  Pallas kernels  70.1 us (94%)
  local copies, waits for them, and re-layouts  3.52 us (5%)
    pallas_call x1, Pallas kernels, local(): pl.pallas_call(kernel, out_shape=(vm(N, N, N), vm(N, N, N), vm(1, STEPS))...  70.1 us
    unnamed x3, local copies, waits for them, and re-layouts  3.52 us

profile of v5, /device:TPU:0, one launch (start us, length us, event | category | flops | bytes accessed | tf_op | source)
XLA Modules:
  0.0 74.3 jit_solution(6552630791927666148)
XLA Ops:
  0.6 70.1 %shard_map.67 = (f32[72,72,72]{2,1,0:T(8,128)S(1)}, f32[72,72,72]{2,1,0:T(8,128)S(1)}, f32[1,8]{1,0:T(1,128)S(1)}) custom-call(f32[72,72,72]{2,1,0:T(8,128)} %k_hbm.1, f32[72,72,72]{2,1,0:T(8,128)} %f_hbm.1, f32[72,72,72]{2,1,0:T(8,128)} %u_hbm.1, f32[6,144,144]{2,1,0:T(8,128)} %kg_hbm.1), custom_call_target="tpu_custom_call" | custom-call | tf_op jit(solution)/shard_map/pallas_call | solution.py:749
  70.7 1.5 %copy.10 = f32[72,72,72]{2,1,0:T(8,128)} copy(f32[72,72,72]{2,1,0:T(8,128)S(1)} %get-tuple-element.9) | data formatting | bytes 2985984
  72.2 0.5 copy.12
  72.8 1.5 %copy.11 = f32[72,72,72]{2,1,0:T(8,128)} copy(f32[72,72,72]{2,1,0:T(8,128)S(1)} %get-tuple-element.10) | data formatting | bytes 2985984

commit v6 on v5

--- a/solution.py
+++ b/solution.py
@@ -316,7 +316,7 @@
                 out = x if t == 0 else pick(slots == t, x, out)
             lane_s[n, o] = out
         return carry
-    lax.fori_loop(0, TILES, pack_one, 0)
+    planes(0, TILES, pack_one, 0, 3)
     pl.semaphore_wait(barrier, len(OTHERS))
     one_x = [send(0, k_in.at[pl.ds(last_x, 1)], kx, (1, 0, 0)), send(1, u_in.at[pl.ds(last_x, 1)], ux, (1, 0, 0))]
     one_y = send(2, row_s, row_r, (0, 1, 0))
@@ -355,6 +355,14 @@
         return carry
     planes(0, N, take_f, 0)
 
+    def lay_out(i, carry):
+        side = jnp.concatenate([pick(at_wall, wall_column(i, jt), ones) for jt in range(TILES)], axis=0)
+        for nat, src, rest in ((k_nat, k_in, side), (u_nat, u_in, jnp.zeros((N, LANES), F32))):
+            nat[i, 0:N, N:] = rest[:, N:]
+            nat[i, 0:N, 0:N] = src[i]
+        return carry
+    planes(0, N, lay_out, 0)
+
     u_nat[E - UNIT - LAST * cx] = jnp.zeros((E, LANES), F32)
     one_lane = N + 55 * cz
     at_one = lane == one_lane
@@ -364,17 +372,11 @@
     k_nat[E + UNIT, 0:N, 0:N] = kx[0]
 
     def unpack_one(o, carry):
-        lanes_in = [turn(lane_r[n, o], one_lane - (N - UNIT - last_z)) for n in range(2)]
-        for pi in range(SUB):
-            i = o * SUB + pi
-            planes_in = [widen(k_in[i]), widen(u_in[i])]
-            for n, nat in enumerate((k_nat, u_nat)):
-                out = []
-                for jt in range(TILES):
-                    other = zero if n else pick(at_wall, wall_column(i, jt), ones)
-                    other = pick(at_one, shift(lanes_in[n], -(pi * TILES + jt)), other)
-                    out.append(pick(own_lane, planes_in[n][SUB * jt:SUB * jt + SUB], other))
-                nat[i, 0:N, :] = jnp.concatenate(out, axis=0)
+        for n, nat in enumerate((k_nat, u_nat)):
+            got = turn(lane_r[n, o], one_lane - (N - 1 - last_z))
+            for t in range(N):
+                here = nat.at[o * SUB + t // TILES, pl.ds(SUB * (t % TILES), SUB), :]
+                pltpu.store(here, shift(got, -t), mask=at_one)
         return carry
     lax.fori_loop(0, TILES, unpack_one, 0)
 
@@ -460,7 +462,7 @@
         cy_a[p] = harmonic(high, low)
         cz_a[p] = harmonic(kc, lane_down(kc))
         return carry
-    planes(0, E, faces, 0)
+    planes(0, E, faces, 0, SUB)
     cx_a[E] = cx_a[0]
     cx_a[E + UNIT] = cx_a[1]
 
@@ -473,8 +475,8 @@
             for b in range(NB):
                 k_nat[p, pl.ds(SUB * b, SUB), :] = sd[b] if b < 2 else pick(row72, zero, sd[b])
         return carry
-    planes(0, N, functools.partial(scales, True), 0)
-    planes(N, E, functools.partial(scales, False), 0)
+    planes(0, N, functools.partial(scales, True), 0, SUB)
+    planes(N, E, functools.partial(scales, False), 0, SUB)
 
     for copy in (z_y, z_z, z_d):
         copy.wait()

time: 74.4 us -> 75 us (level)
  no operation moved by 1% of the time
where the time goes in v6:
time: 75 us; the launch traced here: 74.9 us
  Pallas kernels  70.7 us (94%)
  local copies, waits for them, and re-layouts  3.52 us (5%)
    pallas_call x1, Pallas kernels, local(): pl.pallas_call(kernel, out_shape=(vm(N, N, N), vm(N, N, N), vm(1, STEPS))...  70.7 us
    unnamed x3, local copies, waits for them, and re-layouts  3.52 us

profile of v6, /device:TPU:0, one launch (start us, length us, event | category | flops | bytes accessed | tf_op | source)
XLA Modules:
  0.0 74.9 jit_solution(6748073881642191614)
XLA Ops:
  0.6 70.7 %shard_map.67 = (f32[72,72,72]{2,1,0:T(8,128)S(1)}, f32[72,72,72]{2,1,0:T(8,128)S(1)}, f32[1,8]{1,0:T(1,128)S(1)}) custom-call(f32[72,72,72]{2,1,0:T(8,128)} %k_hbm.1, f32[72,72,72]{2,1,0:T(8,128)} %f_hbm.1, f32[72,72,72]{2,1,0:T(8,128)} %u_hbm.1, f32[6,144,144]{2,1,0:T(8,128)} %kg_hbm.1), custom_call_target="tpu_custom_call" | custom-call | tf_op jit(solution)/shard_map/pallas_call | solution.py:751
  71.4 1.5 %copy.10 = f32[72,72,72]{2,1,0:T(8,128)} copy(f32[72,72,72]{2,1,0:T(8,128)S(1)} %get-tuple-element.9) | data formatting | bytes 2985984
  72.9 0.5 copy.12
  73.4 1.5 %copy.11 = f32[72,72,72]{2,1,0:T(8,128)} copy(f32[72,72,72]{2,1,0:T(8,128)S(1)} %get-tuple-element.10) | data formatting | bytes 2985984

commit v7 on v6

--- a/solution.py
+++ b/solution.py
@@ -253,7 +253,7 @@
     def widen(x):
         return x if x.shape[1] == LANES else jnp.concatenate([x, jnp.zeros((x.shape[0], LANES - x.shape[1]), F32)], axis=1)
 
-    def pack(nat, packed, corner):
+    def pack(nat, packed, corner, lo, hi):
         group8 = lax.rem(lane + (LANES - src8), LANES) // SUB
         groups = [group8 == g for g in range(GROUPS)]
 
@@ -274,7 +274,7 @@
                 out = x if g == 0 else pick(groups[g], x, out)
             corner[o] = out
             return carry
-        lax.fori_loop(0, TILES, body, 0)
+        lax.fori_loop(lo, hi, body, 0)
 
     def unpack(own, side, nat, packed, corner, fill, wall, o, carry):
         by = dst8 - (N - H - src8)
@@ -322,7 +322,7 @@
     one_y = send(2, row_s, row_r, (0, 1, 0))
     one_z = send(3, lane_s, lane_r, (0, 0, 1))
     k_y = send(4, k_in.at[:, pl.ds(near_y, SUB), :], ky, (0, 1, 0))
-    pack(k_in, zs.at[0], ds_.at[0])
+    pack(k_in, zs.at[0], ds_.at[0], 0, TILES)
     k_z = send(PIECES, zs.at[0], zr.at[0], (0, 0, 1))
     k_d = send(6, ds_.at[0], dr.at[0], (0, 1, 1))
 
@@ -434,12 +434,15 @@
                 else:
                     z_nat[p, pl.ds(b, LAST, stride=NB), :] = z0[b, :LAST]
         return carry
-    lax.fori_loop(0, N // WIDTH, start_own, 0)
-
-    z_y = send(LAST, z_nat.at[pl.ds(0, N), pl.ds(near_y, SUB), :], z_nat.at[pl.ds(0, N), pl.ds(N, SUB), :], (0, 1, 0))
-    pack(z_nat, zs.at[1], ds_.at[1])
-    z_z = send(8, zs.at[1], zr.at[1], (0, 0, 1))
-    z_d = send(9, ds_.at[1], dr.at[1], (0, 1, 1))
+    z_copies = []
+    for q in range(3):
+        lax.fori_loop(6 * q, 6 * q + 6, start_own, 0)
+        rows = pl.ds(PART * q, PART)
+        z_copies.append(send(7 + q, z_nat.at[rows, pl.ds(near_y, SUB), :], z_nat.at[rows, pl.ds(N, SUB), :], (0, 1, 0)))
+        pack(z_nat, zs.at[1], ds_.at[1], 3 * q, 3 * q + 3)
+        lanes = pl.ds(15 * q, 15)
+        z_copies.append(send(12 + q, zs.at[1, lanes], zr.at[1, lanes], (0, 0, 1)))
+    z_copies.append(send(15, ds_.at[1], dr.at[1], (0, 1, 1)))
 
     def spread(n, nat, take):
         take(SUB * (1 - cx), 0)
@@ -478,7 +481,7 @@
     planes(0, N, functools.partial(scales, True), 0, SUB)
     planes(N, E, functools.partial(scales, False), 0, SUB)
 
-    for copy in (z_y, z_z, z_d):
+    for copy in z_copies:
         copy.wait()
     z_x = spread(11, z_nat, functools.partial(unpack, z_nat, z_nat.at[:, pl.ds(N, SUB), :], z_nat, zr.at[1], dr.at[1],
                                               zero, None))
@@ -762,7 +765,7 @@
                 vm(2, N, N), vm(2, N, N), vm(2, TILES, SUB, LANES), vm(2, TILES, SUB, LANES),
                 vm(NDOT, SUB, LANES), vm(SUB, 2 * NDOT, LANES), vm(SUB, SUB, LANES), vm(SUB, SUB, LANES), vm(44, SUB, LANES),
                 pltpu.SemaphoreType.DMA((6, 3)),
-                pltpu.SemaphoreType.DMA((12,)), pltpu.SemaphoreType.DMA((12,)),
+                pltpu.SemaphoreType.DMA((16,)), pltpu.SemaphoreType.DMA((16,)),
                 pltpu.SemaphoreType.DMA((2, LAST)), pltpu.SemaphoreType.DMA((2, LAST)),
             ],
             compiler_params=pltpu.CompilerParams(collective_id=0, has_side_effects=True, vmem_limit_bytes=57 << 20),

time: 75 us -> 73 us (0.973)
  Pallas kernels: 70.7 us -> 68.8 us
    pallas_call x1, Pallas kernels: 70.7 us -> 68.8 us  [local(): pl.pallas_call(kernel, out_shape=(vm(N, N, N), vm(N, N, N), vm(1, STEPS))...]
where the time goes in v7:
time: 73 us; the launch traced here: 72.9 us
  Pallas kernels  68.8 us (94%)
  local copies, waits for them, and re-layouts  3.52 us (5%)
    pallas_call x1, Pallas kernels, local(): pl.pallas_call(kernel, out_shape=(vm(N, N, N), vm(N, N, N), vm(1, STEPS))...  68.8 us
    unnamed x3, local copies, waits for them, and re-layouts  3.52 us

profile of v7, /device:TPU:0, one launch (start us, length us, event | category | flops | bytes accessed | tf_op | source)
XLA Modules:
  0.0 72.9 jit_solution(9438246526356777460)
XLA Ops:
  0.6 68.8 %shard_map.67 = (f32[72,72,72]{2,1,0:T(8,128)S(1)}, f32[72,72,72]{2,1,0:T(8,128)S(1)}, f32[1,8]{1,0:T(1,128)S(1)}) custom-call(f32[72,72,72]{2,1,0:T(8,128)} %k_hbm.1, f32[72,72,72]{2,1,0:T(8,128)} %f_hbm.1, f32[72,72,72]{2,1,0:T(8,128)} %u_hbm.1, f32[6,144,144]{2,1,0:T(8,128)} %kg_hbm.1), custom_call_target="tpu_custom_call" | custom-call | tf_op jit(solution)/shard_map/pallas_call | solution.py:754
  69.4 1.5 %copy.10 = f32[72,72,72]{2,1,0:T(8,128)} copy(f32[72,72,72]{2,1,0:T(8,128)S(1)} %get-tuple-element.9) | data formatting | bytes 2985984
  70.9 0.5 copy.12
  71.4 1.5 %copy.11 = f32[72,72,72]{2,1,0:T(8,128)} copy(f32[72,72,72]{2,1,0:T(8,128)S(1)} %get-tuple-element.10) | data formatting | bytes 2985984

commit v8 on v7

--- a/solution.py
+++ b/solution.py
@@ -28,6 +28,7 @@
 ZERO, ONE, HALF, TWO = 0.0, 1.0, 0.5, 2.0
 UNIT = 1
 HEAD = 4
+PAIR = 2
 
 
 def iota(axis):
@@ -403,17 +404,17 @@
         return ((h_x + h_xn) + (h_y + row_up(h_y))) + (h_z + lane_up(h_z))
 
     def start_own(n, carry):
-        p0 = WIDTH * n
-        first_trip, last_trip = n == 0, n == N // WIDTH - UNIT
+        p0 = PAIR * n
+        first_trip, last_trip = n == 0, n == N // PAIR - UNIT
         k_p = [load_chunk(k_nat, jnp.where(first_trip, E + cx, p0 - UNIT))]
         u_p = [load_chunk(u_nat, jnp.where(first_trip, E - UNIT, p0 - UNIT))]
-        for w in range(WIDTH):
+        for w in range(PAIR):
             k_p.append(load_chunk(k_nat, p0 + w))
             u_p.append(load_chunk(u_nat, p0 + w))
-        k_p.append(load_chunk(k_nat, jnp.where(last_trip, E + UNIT - cx, p0 + WIDTH)))
-        u_p.append(load_chunk(u_nat, p0 + WIDTH))
-        h_x = [harmonic(k_p[w + UNIT], k_p[w]) for w in range(WIDTH + UNIT)]
-        for w in range(WIDTH):
+        k_p.append(load_chunk(k_nat, jnp.where(last_trip, E + UNIT - cx, p0 + PAIR)))
+        u_p.append(load_chunk(u_nat, p0 + PAIR))
+        h_x = [harmonic(k_p[w + UNIT], k_p[w]) for w in range(PAIR + UNIT)]
+        for w in range(PAIR):
             p, kc = p0 + w, k_p[w + UNIT]
             wall, got = full(wy[pl.ds(p, 1), :]), full(row_r[0, pl.ds(p, 1), :])
             low = replace(row_down(kc), 0, row0, jnp.where(cy == 0, wall, got))
@@ -436,7 +437,7 @@
         return carry
     z_copies = []
     for q in range(3):
-        lax.fori_loop(6 * q, 6 * q + 6, start_own, 0)
+        lax.fori_loop(12 * q, 12 * q + 12, start_own, 0)
         rows = pl.ds(PART * q, PART)
         z_copies.append(send(7 + q, z_nat.at[rows, pl.ds(near_y, SUB), :], z_nat.at[rows, pl.ds(N, SUB), :], (0, 1, 0)))
         pack(z_nat, zs.at[1], ds_.at[1], 3 * q, 3 * q + 3)
@@ -550,8 +551,9 @@
     at_edge = lane == N * cz
 
     def wrap(ref):
-        ref[0] = ref[E]
+        ref[0] = jnp.where(cx == 0, ref[1], ref[E])
         ref[E + UNIT] = ref[1]
+        ref[N + UNIT] = jnp.where(cx == 1, ref[N], ref[N + UNIT])
 
     sums = lax.fori_loop(0, 14, lambda n, carry: first(True, PIECES, 1 + PIECES * n, carry), (zero,) * 6)
     z_x.wait()
@@ -597,7 +599,8 @@
     for k in range(1, STEPS):
         sums = lax.fori_loop(0, N // SUB, lambda n, carry: advance(k, True, SUB, SUB * n, carry), (zero,) * 6)
         if k < STEPS - UNIT:
-            advance(k, False, SUB, N, ())
+            depth = (STEPS - k) // PAIR * PAIR
+            advance(k, False, depth, N + (H - depth) * cx, ())
             wrap(b_a[k])
         acc[1 + k] = own_cells(sums[0], sums[1])
         acc[GROUPS + k - UNIT] = own_cells(sums[2], sums[3])

time: 73 us -> 73.7 us (level)
  no operation moved by 1% of the time
where the time goes in v8:
time: 73.7 us; the launch traced here: 73.6 us
  Pallas kernels  69.5 us (94%)
  local copies, waits for them, and re-layouts  3.52 us (5%)
    pallas_call x1, Pallas kernels, local(): pl.pallas_call(kernel, out_shape=(vm(N, N, N), vm(N, N, N), vm(1, STEPS))...  69.5 us
    unnamed x3, local copies, waits for them, and re-layouts  3.52 us

profile of v8, /device:TPU:0, one launch (start us, length us, event | category | flops | bytes accessed | tf_op | source)
XLA Modules:
  0.0 73.6 jit_solution(9447075821770282018)
XLA Ops:
  0.6 69.5 %shard_map.67 = (f32[72,72,72]{2,1,0:T(8,128)S(1)}, f32[72,72,72]{2,1,0:T(8,128)S(1)}, f32[1,8]{1,0:T(1,128)S(1)}) custom-call(f32[72,72,72]{2,1,0:T(8,128)} %k_hbm.1, f32[72,72,72]{2,1,0:T(8,128)} %f_hbm.1, f32[72,72,72]{2,1,0:T(8,128)} %u_hbm.1, f32[6,144,144]{2,1,0:T(8,128)} %kg_hbm.1), custom_call_target="tpu_custom_call" | custom-call | tf_op jit(solution)/shard_map/pallas_call | solution.py:757
  70.1 1.5 %copy.10 = f32[72,72,72]{2,1,0:T(8,128)} copy(f32[72,72,72]{2,1,0:T(8,128)S(1)} %get-tuple-element.9) | data formatting | bytes 2985984
  71.6 0.5 copy.12
  72.1 1.5 %copy.11 = f32[72,72,72]{2,1,0:T(8,128)} copy(f32[72,72,72]{2,1,0:T(8,128)S(1)} %get-tuple-element.10) | data formatting | bytes 2985984

commit v9 on v7

--- a/solution.py
+++ b/solution.py
@@ -28,6 +28,7 @@
 ZERO, ONE, HALF, TWO = 0.0, 1.0, 0.5, 2.0
 UNIT = 1
 HEAD = 4
+PAIR = 2
 
 
 def iota(axis):
@@ -550,8 +551,9 @@
     at_edge = lane == N * cz
 
     def wrap(ref):
-        ref[0] = ref[E]
+        ref[0] = jnp.where(cx == 0, ref[1], ref[E])
         ref[E + UNIT] = ref[1]
+        ref[N + UNIT] = jnp.where(cx == 1, ref[N], ref[N + UNIT])
 
     sums = lax.fori_loop(0, 14, lambda n, carry: first(True, PIECES, 1 + PIECES * n, carry), (zero,) * 6)
     z_x.wait()
@@ -597,7 +599,8 @@
     for k in range(1, STEPS):
         sums = lax.fori_loop(0, N // SUB, lambda n, carry: advance(k, True, SUB, SUB * n, carry), (zero,) * 6)
         if k < STEPS - UNIT:
-            advance(k, False, SUB, N, ())
+            depth = (STEPS - k) // PAIR * PAIR
+            advance(k, False, depth, N + (H - depth) * cx, ())
             wrap(b_a[k])
         acc[1 + k] = own_cells(sums[0], sums[1])
         acc[GROUPS + k - UNIT] = own_cells(sums[2], sums[3])

time: 73 us -> 72.6 us (level)
  no operation moved by 1% of the time
where the time goes in v9:
time: 72.6 us; the launch traced here: 72.5 us
  Pallas kernels  68.3 us (94%)
  local copies, waits for them, and re-layouts  3.52 us (5%)
    pallas_call x1, Pallas kernels, local(): pl.pallas_call(kernel, out_shape=(vm(N, N, N), vm(N, N, N), vm(1, STEPS))...  68.3 us
    unnamed x3, local copies, waits for them, and re-layouts  3.52 us

profile of v9, /device:TPU:0, one launch (start us, length us, event | category | flops | bytes accessed | tf_op | source)
XLA Modules:
  0.0 72.5 jit_solution(14915838452697639224)
XLA Ops:
  0.6 68.3 %shard_map.67 = (f32[72,72,72]{2,1,0:T(8,128)S(1)}, f32[72,72,72]{2,1,0:T(8,128)S(1)}, f32[1,8]{1,0:T(1,128)S(1)}) custom-call(f32[72,72,72]{2,1,0:T(8,128)} %k_hbm.1, f32[72,72,72]{2,1,0:T(8,128)} %f_hbm.1, f32[72,72,72]{2,1,0:T(8,128)} %u_hbm.1, f32[6,144,144]{2,1,0:T(8,128)} %kg_hbm.1), custom_call_target="tpu_custom_call" | custom-call | tf_op jit(solution)/shard_map/pallas_call | solution.py:757
  69.0 1.5 %copy.10 = f32[72,72,72]{2,1,0:T(8,128)} copy(f32[72,72,72]{2,1,0:T(8,128)S(1)} %get-tuple-element.9) | data formatting | bytes 2985984
  70.5 0.5 copy.12
  71.0 1.5 %copy.11 = f32[72,72,72]{2,1,0:T(8,128)} copy(f32[72,72,72]{2,1,0:T(8,128)S(1)} %get-tuple-element.10) | data formatting | bytes 2985984

commit v10 on v9

--- a/solution.py
+++ b/solution.py
@@ -254,7 +254,7 @@
     def widen(x):
         return x if x.shape[1] == LANES else jnp.concatenate([x, jnp.zeros((x.shape[0], LANES - x.shape[1]), F32)], axis=1)
 
-    def pack(nat, packed, corner, lo, hi):
+    def pack(nat, packed, corner, lo, hi, width):
         group8 = lax.rem(lane + (LANES - src8), LANES) // SUB
         groups = [group8 == g for g in range(GROUPS)]
 
@@ -275,7 +275,7 @@
                 out = x if g == 0 else pick(groups[g], x, out)
             corner[o] = out
             return carry
-        lax.fori_loop(lo, hi, body, 0)
+        planes(lo, hi, body, 0, width)
 
     def unpack(own, side, nat, packed, corner, fill, wall, o, carry):
         by = dst8 - (N - H - src8)
@@ -323,7 +323,7 @@
     one_y = send(2, row_s, row_r, (0, 1, 0))
     one_z = send(3, lane_s, lane_r, (0, 0, 1))
     k_y = send(4, k_in.at[:, pl.ds(near_y, SUB), :], ky, (0, 1, 0))
-    pack(k_in, zs.at[0], ds_.at[0], 0, TILES)
+    pack(k_in, zs.at[0], ds_.at[0], 0, TILES, UNIT)
     k_z = send(PIECES, zs.at[0], zr.at[0], (0, 0, 1))
     k_d = send(6, ds_.at[0], dr.at[0], (0, 1, 1))
 
@@ -440,7 +440,7 @@
         lax.fori_loop(6 * q, 6 * q + 6, start_own, 0)
         rows = pl.ds(PART * q, PART)
         z_copies.append(send(7 + q, z_nat.at[rows, pl.ds(near_y, SUB), :], z_nat.at[rows, pl.ds(N, SUB), :], (0, 1, 0)))
-        pack(z_nat, zs.at[1], ds_.at[1], 3 * q, 3 * q + 3)
+        pack(z_nat, zs.at[1], ds_.at[1], 3 * q, 3 * q + 3, 3)
         lanes = pl.ds(15 * q, 15)
         z_copies.append(send(12 + q, zs.at[1, lanes], zr.at[1, lanes], (0, 0, 1)))
     z_copies.append(send(15, ds_.at[1], dr.at[1], (0, 1, 1)))

time: 72.6 us -> 72.2 us (level)
  no operation moved by 1% of the time
where the time goes in v10:
time: 72.2 us; the launch traced here: 72.1 us
  Pallas kernels  67.9 us (94%)
  local copies, waits for them, and re-layouts  3.52 us (5%)
    pallas_call x1, Pallas kernels, local(): pl.pallas_call(kernel, out_shape=(vm(N, N, N), vm(N, N, N), vm(1, STEPS))...  67.9 us
    unnamed x3, local copies, waits for them, and re-layouts  3.52 us

profile of v10, /device:TPU:0, one launch (start us, length us, event | category | flops | bytes accessed | tf_op | source)
XLA Modules:
  0.0 72.1 jit_solution(6231475645536394130)
XLA Ops:
  0.6 67.9 %shard_map.67 = (f32[72,72,72]{2,1,0:T(8,128)S(1)}, f32[72,72,72]{2,1,0:T(8,128)S(1)}, f32[1,8]{1,0:T(1,128)S(1)}) custom-call(f32[72,72,72]{2,1,0:T(8,128)} %k_hbm.1, f32[72,72,72]{2,1,0:T(8,128)} %f_hbm.1, f32[72,72,72]{2,1,0:T(8,128)} %u_hbm.1, f32[6,144,144]{2,1,0:T(8,128)} %kg_hbm.1), custom_call_target="tpu_custom_call" | custom-call | tf_op jit(solution)/shard_map/pallas_call | solution.py:757
  68.6 1.5 %copy.10 = f32[72,72,72]{2,1,0:T(8,128)} copy(f32[72,72,72]{2,1,0:T(8,128)S(1)} %get-tuple-element.9) | data formatting | bytes 2985984
  70.1 0.5 copy.12
  70.6 1.5 %copy.11 = f32[72,72,72]{2,1,0:T(8,128)} copy(f32[72,72,72]{2,1,0:T(8,128)S(1)} %get-tuple-element.10) | data formatting | bytes 2985984

commit v11 on v10

--- a/solution.py
+++ b/solution.py
@@ -16,6 +16,7 @@
 MESH = pl.DeviceIdType.MESH
 F32 = jnp.float32
 OTHERS = [(fx, fy, fz) for fx in (0, 1) for fy in (0, 1) for fz in (0, 1) if fx or fy or fz]
+OTHERS.sort(key=lambda flips: -sum(flips[1:]))
 NDOT = 24
 SUB = 8
 LANES = 128

time: 72.2 us -> 72.2 us (level)
  no operation moved by 1% of the time
where the time goes in v11:
time: 72.2 us; the launch traced here: 72.1 us
  Pallas kernels  67.9 us (94%)
  local copies, waits for them, and re-layouts  3.52 us (5%)
    pallas_call x1, Pallas kernels, local(): pl.pallas_call(kernel, out_shape=(vm(N, N, N), vm(N, N, N), vm(1, STEPS))...  67.9 us
    unnamed x3, local copies, waits for them, and re-layouts  3.52 us

profile of v11, /device:TPU:0, one launch (start us, length us, event | category | flops | bytes accessed | tf_op | source)
XLA Modules:
  0.0 72.1 jit_solution(5750269932766148387)
XLA Ops:
  0.6 67.9 %shard_map.67 = (f32[72,72,72]{2,1,0:T(8,128)S(1)}, f32[72,72,72]{2,1,0:T(8,128)S(1)}, f32[1,8]{1,0:T(1,128)S(1)}) custom-call(f32[72,72,72]{2,1,0:T(8,128)} %k_hbm.1, f32[72,72,72]{2,1,0:T(8,128)} %f_hbm.1, f32[72,72,72]{2,1,0:T(8,128)} %u_hbm.1, f32[6,144,144]{2,1,0:T(8,128)} %kg_hbm.1), custom_call_target="tpu_custom_call" | custom-call | tf_op jit(solution)/shard_map/pallas_call | solution.py:758
  68.6 1.5 %copy.10 = f32[72,72,72]{2,1,0:T(8,128)} copy(f32[72,72,72]{2,1,0:T(8,128)S(1)} %get-tuple-element.9) | data formatting | bytes 2985984
  70.1 0.5 copy.12
  70.6 1.5 %copy.11 = f32[72,72,72]{2,1,0:T(8,128)} copy(f32[72,72,72]{2,1,0:T(8,128)S(1)} %get-tuple-element.10) | data formatting | bytes 2985984
